TPU v7x, 512 devices: a whole 4x4x16 slice. The times are simulated.
512 devices in a mesh: ctx: 64 (over x, z_hi, y), ch: 8 (over z_lo, core).
Axes of the slice: x: 4, y: 4, z: 16 (z_hi: 4, z_lo: 4; z = z_hi * 4 + z_lo), core: 2. Of those that a mesh axis runs over, the one named last changes fastest.
Arguments:
- value_in: bfloat16 [8192, 4096], P('ctx', 'ch'), may hold values from -6 to 6
- key_in: bfloat16 [8192, 4096], P('ctx', 'ch'), may hold values from -6 to 6
- gate_short: bfloat16 [8192, 4096], P('ctx', 'ch'), may hold values from -6 to 6
- gate_long: bfloat16 [8192, 4096], P('ctx', 'ch'), may hold values from -6 to 6
- short_filter: bfloat16 [256, 128], P('ch'), may hold values from -0.5 to 0.5
- long_filter: float32 [4096, 8192], P(('ch', 'ctx')), may hold values from -2 to 2
- skip_gain: float32 [4096], P('ch'), may hold values from 0.5 to 1.5
- out_weight: bfloat16 [4096, 4096], P('ctx', 'ch'), may hold values from -0.09375 to 0.09375
Outputs:
- layer_out: bfloat16 [8192, 4096], P('ctx', 'ch')
All inputs are finite; a program needn't handle non-finite values.
Results may differ from a plain program's by a relative error of at most 0.0067.
Values may be sent and summed in bfloat16 or wider, within the bound.
No kernel may reach another device: no remote copies, remote signals or barrier semaphores. Data moves between devices by JAX's collectives and lax.ppermute only.
A program may use at most 64 MiB of HBM per device.

v0:
```python
import math

import jax
import jax.numpy as jnp
from jax import lax
from jax.sharding import PartitionSpec as P


def passed_along(value, axis, steps):
    count = lax.axis_size(axis)
    first, last = (max(0, -steps), min(count, count - steps))
    return lax.ppermute(value, axis, [(source, source + steps) for source in range(first, last)])


def split_up(shard, dim, size):
    dims = shard.shape
    parts = shard.reshape(*dims[:dim], size, dims[dim] // size, *dims[dim + 1 :])
    return jnp.moveaxis(parts, dim, 0)


def piece_ends(length, count):
    unit = 8 if length >= 8 * count else 1
    return [length // unit * k // count * unit for k in range(1, count)]


def in_order(parts, dim):
    dims = list(parts.shape[1:])
    dims[dim] *= parts.shape[0]
    return jnp.moveaxis(parts, 0, dim).reshape(dims)


def cut_exchange(shard, axis, pieces, split_dim, concat_dim):
    parts = split_up(shard, split_dim, lax.axis_size(axis))
    widest = max(range(1, max(2, parts.ndim - 1)), key=lambda d: parts.shape[d])
    gathered = []
    for piece in jnp.split(parts, piece_ends(parts.shape[widest], pieces), axis=widest):
        if piece.size:
            gathered.append(lax.all_to_all(piece, axis, split_axis=0, concat_axis=0, tiled=True))
    return in_order(jnp.concatenate(gathered, axis=widest), concat_dim)


def sent_to_all(shard, axis):
    size = lax.axis_size(axis)
    return lax.all_to_all(
        jnp.broadcast_to(shard[None], (size, *shard.shape)), axis, 0, 0, tiled=True
    )


def gathered_copies(shard, axis, dim):
    return in_order(sent_to_all(shard, axis), dim)


def toeplitz(tap_rows, width):
    group_count, tap_count = tap_rows.shape
    band_width = width + tap_count - 1
    band_line = jnp.concatenate(
        [
            jnp.zeros((group_count, width), tap_rows.dtype),
            tap_rows[:, ::-1],
            jnp.zeros((group_count, width), tap_rows.dtype),
        ],
        1,
    )
    line_len = band_line.shape[1]
    row_span = line_len - 1
    tiled = jnp.tile(band_line, (1, width))[:, : width * row_span].reshape(
        group_count, width, row_span
    )
    return tiled[:, :, width : width + band_width]


def short_blocks(padded, tap_rows, width):
    group_count, group_width, extended = padded.shape
    tap_count = tap_rows.shape[1]
    seq_len = extended - (tap_count - 1)
    block_count = seq_len // width
    inner_rows = padded[:, :, tap_count - 1 :].reshape(group_count, group_width, block_count, width)
    earlier = padded[:, :, :seq_len].reshape(group_count, group_width, block_count, width)[
        :, :, :, : tap_count - 1
    ]
    windows = jnp.concatenate([earlier, inner_rows], -1)
    band = toeplitz(tap_rows, width)
    result = jnp.einsum("gte,gcbe->gcbt", band, windows, preferred_element_type=jnp.float32)
    return result.reshape(group_count, group_width, seq_len)


def tables(size):
    counter = jnp.arange(size, dtype=jnp.int32)
    angle = 2.0 * math.pi / size * (counter[:, None] * counter[None, :] % size).astype(jnp.float32)
    return (jnp.cos(angle), jnp.sin(angle))


def left_mul(matrix, signal):
    return jnp.einsum("kn,cnq->ckq", matrix, signal, precision=lax.Precision.HIGHEST)


def right_mul(signal, matrix):
    return jnp.einsum("ckn,nq->ckq", signal, matrix, precision=lax.Precision.HIGHEST)


def long_conv(local_rows, long_filter):
    rows, seq_len = local_rows.shape
    span_len = 2 * seq_len
    second_len = min(2 ** ((span_len.bit_length() - 1) // 2), span_len & -span_len)
    first_len = span_len // second_len
    cos_p, sin_p = tables(first_len)
    cos_q, sin_q = tables(second_len)
    first_idx = jnp.arange(first_len, dtype=jnp.int32)
    second_idx = jnp.arange(second_len, dtype=jnp.int32)
    twist_angle = (
        2.0
        * math.pi
        / span_len
        * (first_idx[:, None] * second_idx[None, :] % span_len).astype(jnp.float32)
    )
    twist_re = jnp.cos(twist_angle)
    twist_im = jnp.sin(twist_angle)

    def spectrum(signal):
        shaped = jnp.concatenate([signal, jnp.zeros_like(signal)], 1).reshape(
            rows, first_len, second_len
        )
        section_re = left_mul(cos_p, shaped)
        section_im = -left_mul(sin_p, shaped)
        turned_re = section_re * twist_re + section_im * twist_im
        turned_im = section_im * twist_re - section_re * twist_im
        final_re = right_mul(turned_re, cos_q) + right_mul(turned_im, sin_q)
        final_im = right_mul(turned_im, cos_q) - right_mul(turned_re, sin_q)
        return (final_re, final_im)

    data_re, data_im = spectrum(local_rows.astype(jnp.float32))
    filt_re, filt_im = spectrum(long_filter)
    prod_re = data_re * filt_re - data_im * filt_im
    prod_im = data_re * filt_im + data_im * filt_re
    back_re = right_mul(prod_re, cos_q) - right_mul(prod_im, sin_q)
    back_im = right_mul(prod_im, cos_q) + right_mul(prod_re, sin_q)
    untwist_re = back_re * twist_re - back_im * twist_im
    untwist_im = back_re * twist_im + back_im * twist_re
    signal_out = (left_mul(cos_p, untwist_re) - left_mul(sin_p, untwist_im)) / span_len
    return signal_out.reshape(rows, span_len)[:, :seq_len].astype(jnp.bfloat16)


def shards(
    value_in, key_in, gate_short, gate_long, short_filter, long_filter, skip_gain, out_weight
):
    tok_rows, channels = value_in.shape
    ctx_ways = lax.axis_size("ctx")
    per_dev = channels // ctx_ways
    seq_len = tok_rows * ctx_ways
    tap_count = short_filter.shape[1]
    group_size = channels // short_filter.shape[0]
    weight_cols = lax.all_gather(out_weight, "ctx", axis=0, tiled=True)
    product = (value_in.astype(jnp.float32) * key_in.astype(jnp.float32)).astype(jnp.bfloat16).T
    gate_rows = gate_short.T
    prior_rim = passed_along(product, "ctx", 1)
    extended = jnp.concatenate([prior_rim[:, 1:], product], 1)
    short_out = short_blocks(
        extended.reshape(channels // group_size, group_size, tok_rows + tap_count - 1),
        short_filter,
        min(512, tok_rows),
    ).reshape(channels, tok_rows)
    mid_rows = (gate_rows.astype(jnp.float32) * short_out).astype(jnp.bfloat16)
    regrouped = lax.all_to_all(
        mid_rows.reshape(ctx_ways, per_dev, tok_rows),
        "ctx",
        split_axis=0,
        concat_axis=2,
        tiled=True,
    )
    long_part = long_conv(regrouped.reshape(per_dev, seq_len), long_filter)
    returned = cut_exchange(long_part.reshape(1, per_dev, seq_len), "ctx", 2, 2, 0)
    long_rows = returned.reshape(channels, tok_rows)
    gated_rows = (
        gate_long.T.astype(jnp.float32)
        * (long_rows.astype(jnp.float32) + skip_gain[:, None] * mid_rows.astype(jnp.float32))
    ).astype(jnp.bfloat16)
    features = gathered_copies(gated_rows, "ch", 0)
    projected = lax.dot_general(
        features, weight_cols, (((0,), (0,)), ((), ())), preferred_element_type=jnp.float32
    )
    return projected.astype(jnp.bfloat16)


def solution(mesh):
    in_specs = (
        P("ctx", "ch"),
        P("ctx", "ch"),
        P("ctx", "ch"),
        P("ctx", "ch"),
        P("ch", None),
        P(("ch", "ctx"), None),
        P("ch"),
        P("ctx", "ch"),
    )
    out_specs = P("ctx", "ch")
    return jax.shard_map(shards, mesh=mesh, in_specs=in_specs, out_specs=out_specs, check_vma=False)
```

profile of v0, /device:TPU:1, one launch (start us, length us, event | category | flops | bytes accessed | tf_op | source)
XLA Modules:
  0.0 188.6 jit_solution(6191014609167570638)
XLA Ops:
  6.5 1.0 fusion.31
  7.5 4.0 %collective-permute-start = (bf16[512,128]{0,1:T(8,128)(2,1)S(1)}, bf16[512,128]{0,1:T(8,128)(2,1)S(1)}, u32[]{:S(2)}, u32[]{:S(2)}) collective-permute-start(bf16[512,128]{0,1:T(8,128)(2,1)S(1)} %fusion.31), channel_id=1, source_target_pairs={{0,8},{8,16},{16,24},{24,32},{32,40},{40,48},{48,56},{56,64},{64,7... | collective-permute-start | bytes 393224 | tf_op jit(solution)/shard_map/ppermute | solution.py:12
  11.6 1.0 pad_bitcast_fusion
  12.6 1.2 convolution_bitcast_fusion
  13.8 1.2 fusion.2
  15.0 0.3 fusion.67
  15.2 0.3 fusion.68
  15.6 0.1 copy.53
  15.7 1.2 fusion.35
  16.9 1.2 convolution_subtract_fusion.2
  18.2 0.3 tile.4
  18.5 1.9 copy.91
  20.4 1.9 %slice.33 = bf16[32,49024]{1,0:T(8,128)(2,1)} slice(bf16[32,49152]{1,0:T(8,128)(2,1)S(1)} %bitcast.119), slice={[0:32], [0:49024]} | slice | bytes 6275072 | tf_op jit(solution)/shard_map/slice | solution.py:66
  22.3 9.3 %reshape.90 = bf16[32,128,383]{2,1,0:T(8,128)(2,1)} reshape(bf16[32,49024]{1,0:T(8,128)(2,1)} %slice.33) | data formatting | bytes 6275072 | tf_op jit(solution)/shard_map/reshape | solution.py:66
  31.6 0.1 copy.50
  31.8 0.1 copy.51
  31.9 0.1 slice_bitcast_fusion.2
  32.0 2.3 %fusion = f32[32,16,128]{2,1,0:T(8,128)S(1)} fusion(bf16[32,128,383]{2,1,0:T(8,128)(2,1)} %reshape.90, bf16[32,16,1,128]{3,1,0,2:T(8,128)(2,1)S(1)} %get-tuple-element.8, bf16[32,16,1,127]{3,1,0,2:T(8,128)(2,1)S(1)} %bitcast.125), kind=kOutput, calls=%fused_computation | convolution fusion | flops 33945600 | bytes 2620416 | tf_op jit(solution)/shard_map/gte,gcbe->gcbt/dot_general | solution.py:83
  34.3 0.7 fusion.24
  35.0 21.4 %all-to-all-start = ((bf16[64,8,128]{2,1,0:T(8,128)(2,1)}), bf16[64,8,128]{2,1,0:T(8,128)(2,1)S(1)}, u32[]{:S(2)}, u32[]{:S(2)}) async-start(bf16[64,8,128]{2,1,0:T(8,128)(2,1)} %bitcast.8), calls=%async_computation | async-start | bytes 262144 | tf_op jit(solution)/shard_map/all_to_all | solution.py:163
  56.4 1.2 fusion.34
  57.6 1.2 convolution_add_fusion.1
  58.8 15.2 %all-to-all-done = bf16[64,8,128]{2,1,0:T(8,128)(2,1)S(1)} async-done(((bf16[64,8,128]{2,1,0:T(8,128)(2,1)}), bf16[64,8,128]{2,1,0:T(8,128)(2,1)S(1)}, u32[]{:S(2)}, u32[]{:S(2)}) %all-to-all-start) | async-done | bytes 131104 | tf_op jit(solution)/shard_map/all_to_all | solution.py:163
  74.0 0.6 fusion.3
  74.6 0.7 convolution_bitcast_fusion.1
  75.3 1.2 fusion.32
  76.5 1.2 fusion.33
  77.7 1.2 convolution_add_fusion.2
  78.9 1.2 multiply_subtract_fusion
  80.1 0.9 fusion.50
  81.0 0.9 fusion.52
  81.9 0.9 convolution_add_fusion
  82.7 1.1 convolution_subtract_fusion.1
  83.9 0.8 fusion.12
  84.7 0.8 fusion.6
  85.5 0.2 copy.70
  85.7 0.2 copy.114
  86.0 0.7 copy.72
  86.6 4.9 %all-to-all-start.2 = ((bf16[64,1,4,128]{3,2,1,0:T(4,128)(2,1)}), bf16[64,1,4,128]{3,2,1,0:T(4,128)(2,1)S(1)}, u32[]{:S(2)}, u32[]{:S(2)}) async-start(bf16[64,1,4,128]{3,2,1,0:T(4,128)(2,1)} %copy.72), calls=%async_computation.2 | async-start | bytes 131072 | tf_op jit(solution)/shard_map/all_to_all | solution.py:38
  91.6 0.7 copy.71
  92.3 15.1 %all-to-all-done.2 = bf16[64,1,4,128]{3,2,1,0:T(4,128)(2,1)S(1)} async-done(((bf16[64,1,4,128]{3,2,1,0:T(4,128)(2,1)}), bf16[64,1,4,128]{3,2,1,0:T(4,128)(2,1)S(1)}, u32[]{:S(2)}, u32[]{:S(2)}) %all-to-all-start.2) | async-done | bytes 65568 | tf_op jit(solution)/shard_map/all_to_all | solution.py:38
  107.4 4.6 %all-to-all-start.1 = ((bf16[64,1,4,128]{3,2,1,0:T(4,128)(2,1)}), bf16[64,1,4,128]{3,2,1,0:T(4,128)(2,1)S(1)}, u32[]{:S(2)}, u32[]{:S(2)}) async-start(bf16[64,1,4,128]{3,2,1,0:T(4,128)(2,1)} %copy.71), calls=%async_computation.1 | async-start | bytes 131072 | tf_op jit(solution)/shard_map/all_to_all | solution.py:38
  112.0 0.1 copy.49
  112.1 17.2 %all-to-all-done.1 = bf16[64,1,4,128]{3,2,1,0:T(4,128)(2,1)S(1)} async-done(((bf16[64,1,4,128]{3,2,1,0:T(4,128)(2,1)}), bf16[64,1,4,128]{3,2,1,0:T(4,128)(2,1)S(1)}, u32[]{:S(2)}, u32[]{:S(2)}) %all-to-all-start.1) | async-done | bytes 65568 | tf_op jit(solution)/shard_map/all_to_all | solution.py:38
  129.3 1.1 fusion.23
  130.4 0.1 broadcast_in_dim.2
  130.5 47.6 %all_to_all.24 = bf16[8,512,128]{2,1,0:T(8,128)(2,1)S(1)} all-to-all(bf16[8,512,128]{2,1,0:T(8,128)(2,1)S(1)} %broadcast_in_dim.2), channel_id=1, replica_groups=mesh['ctx'=64,'ch'=8] {'ch'}, dimensions={0} | all-to-all | bytes 2097152 | tf_op jit(solution)/shard_map/all_to_all | solution.py:44
  178.2 3.6 %convolution_convert_fusion = bf16[128,512]{1,0:T(8,128)(2,1)} fusion(bf16[4096,128]{1,0:T(8,128)(2,1)S(1)} %bitcast.120, bf16[4096,512]{1,0:T(8,128)(2,1)} %all-gather.2.cloned.1.call-done), kind=kOutput, calls=%fused_computation.18 | convolution fusion | flops 536936448 | bytes 5373952 | tf_op jit(solution)/shard_map/dot_general | solution.py:178
  (22 shorter events, 0.4 us)
Async XLA Ops:
  6.5 171.6 %all-gather.2.cloned.1.call-start = ((), (), s32[]{:S(2)}) async-start(), calls=%async_computation.4 | async-start | bytes 4259840 | tf_op jit(solution)/shard_map/all_gather | solution.py:152
  7.5 24.1 %collective-permute-start = (bf16[512,128]{0,1:T(8,128)(2,1)S(1)}, bf16[512,128]{0,1:T(8,128)(2,1)S(1)}, u32[]{:S(2)}, u32[]{:S(2)}) collective-permute-start(bf16[512,128]{0,1:T(8,128)(2,1)S(1)} %fusion.31), channel_id=1, source_target_pairs={{0,8},{8,16},{16,24},{24,32},{32,40},{40,48},{48,56},{56,64},{64,7... | collective-permute-start | bytes 393224 | tf_op jit(solution)/shard_map/ppermute | solution.py:12
  12.6 5.5 %copy-start.2 = (bf16[32,128]{1,0:T(8,128)(2,1)S(1)}, bf16[32,128]{1,0:T(8,128)(2,1)}, u32[]{:S(2)}) copy-start(bf16[32,128]{1,0:T(8,128)(2,1)} %param.12) | copy-start | bytes 24580
  22.3 9.3 %copy-start = (bf16[128,512]{1,0:T(8,128)(2,1)S(1)}, bf16[128,512]{1,0:T(8,128)(2,1)}, u32[]{:S(2)}) copy-start(bf16[128,512]{1,0:T(8,128)(2,1)} %param.10) | copy-start | bytes 393220
  35.0 39.0 %all-to-all-start = ((bf16[64,8,128]{2,1,0:T(8,128)(2,1)}), bf16[64,8,128]{2,1,0:T(8,128)(2,1)S(1)}, u32[]{:S(2)}, u32[]{:S(2)}) async-start(bf16[64,8,128]{2,1,0:T(8,128)(2,1)} %bitcast.8), calls=%async_computation | async-start | bytes 262144 | tf_op jit(solution)/shard_map/all_to_all | solution.py:163
  83.9 28.2 %copy-start.1 = (bf16[128,512]{1,0:T(8,128)(2,1)S(1)}, bf16[128,512]{1,0:T(8,128)(2,1)}, u32[]{:S(2)}) copy-start(bf16[128,512]{1,0:T(8,128)(2,1)} %param.11) | copy-start | bytes 393220
  83.9 45.4 %copy-start.3 = (f32[512]{0:T(512)S(1)}, f32[512]{0:T(512)}, u32[]{:S(2)}) copy-start(f32[512]{0:T(512)} %param.14) | copy-start | bytes 6148
  86.6 20.7 %all-to-all-start.2 = ((bf16[64,1,4,128]{3,2,1,0:T(4,128)(2,1)}), bf16[64,1,4,128]{3,2,1,0:T(4,128)(2,1)S(1)}, u32[]{:S(2)}, u32[]{:S(2)}) async-start(bf16[64,1,4,128]{3,2,1,0:T(4,128)(2,1)} %copy.72), calls=%async_computation.2 | async-start | bytes 131072 | tf_op jit(solution)/shard_map/all_to_all | solution.py:38
  107.4 21.9 %all-to-all-start.1 = ((bf16[64,1,4,128]{3,2,1,0:T(4,128)(2,1)}), bf16[64,1,4,128]{3,2,1,0:T(4,128)(2,1)S(1)}, u32[]{:S(2)}, u32[]{:S(2)}) async-start(bf16[64,1,4,128]{3,2,1,0:T(4,128)(2,1)} %copy.71), calls=%async_computation.1 | async-start | bytes 131072 | tf_op jit(solution)/shard_map/all_to_all | solution.py:38
Sparse Core Ops, SparseCore 0:
  11.7 150.0 all-gather.1
where the time goes:
time: 189 us
  blocking collectives  47.6 us (25%)
  waiting for transfers between devices  47.5 us (25%)
  starting transfers between devices  34.9 us (18%)
  matrix products  24.4 us (13%)
  local copies, waits for them, and re-layouts  17 us (9%)
  between operations  13.7 us (7%)
  other arithmetic  3.34 us (2%)
    all_to_all x1, blocking collectives, sent_to_all(): lax.all_to_all(jnp.broadcast_to(shard[None], (size, *shard.shape)), axis,...  47.6 us
    all_to_all x2, waiting for transfers between devices, cut_exchange(): lax.all_to_all(piece, axis, split_axis=0, concat_axis=0, tiled=True)  32.3 us
    all_to_all x1, starting transfers between devices, shards(): lax.all_to_all(mid_rows.reshape(ctx_ways, per_dev, tok_rows), 'ctx', spli...  21.4 us
    all_to_all x1, waiting for transfers between devices, shards(): lax.all_to_all(mid_rows.reshape(ctx_ways, per_dev, tok_rows), 'ctx', spli...  15.2 us
    dot_general x12, matrix products, right_mul(): jnp.einsum('ckn,nq->ckq', signal, matrix, precision=lax.Precision.HIGHEST)  13.3 us
    all_to_all x2, starting transfers between devices, cut_exchange(): lax.all_to_all(piece, axis, split_axis=0, concat_axis=0, tiled=True)  9.53 us
    reshape x1, local copies, waits for them, and re-layouts, toeplitz(): jnp.tile(band_line, (1, width))[:, :width * row_span]  9.26 us
    dot_general x6, matrix products, left_mul(): jnp.einsum('kn,cnq->ckq', matrix, signal, precision=lax.Precision.HIGHEST)  5.3 us
  transfers between devices with their start and end apart: 5, of which 3 were waited for; matrix products, arithmetic and copies ran while one was open for 21% of the time, Pallas kernels for 0%

commit v1 on v0

v1 whole, which is shorter than its diff:
```python
import jax
import jax.numpy as jnp
from jax import lax
from jax.experimental import pallas as pl
from jax.experimental.pallas import tpu as pltpu
from jax.sharding import Mesh
from jax.sharding import PartitionSpec as P

CTX = ("x", "zh", "y")
CH = ("zl", "core")
LANES = 128
F32 = jnp.float32
BF16 = jnp.bfloat16


def rolled_rows(row):
    square = jnp.broadcast_to(row, (LANES, LANES))
    return pltpu.roll(square, 0, axis=1, stride=1, stride_axis=0)


def upper():
    rows = lax.broadcasted_iota(jnp.int32, (LANES, LANES), 0)
    cols = lax.broadcasted_iota(jnp.int32, (LANES, LANES), 1)
    return cols >= rows


def band_kernel(taps_ref, band_ref):
    own = upper()
    taps = taps_ref[...].astype(F32)
    for g in range(taps_ref.shape[0]):
        turned = rolled_rows(taps[g : g + 1, :])
        band_ref[g, :LANES, :] = jnp.where(own, 0.0, turned).astype(BF16)
        band_ref[g, LANES:, :] = jnp.where(own, turned, 0.0).astype(BF16)


def short_bands(short_filter):
    groups, taps = short_filter.shape
    return pl.pallas_call(
        band_kernel,
        out_shape=jax.ShapeDtypeStruct((groups, 2 * taps, taps), BF16),
        name="short_bands",
        compiler_params=pltpu.CompilerParams(vmem_limit_bytes=8 << 20),
        cost_estimate=pl.CostEstimate(
            flops=2_000_000_000, bytes_accessed=groups * taps * taps * 4, transcendentals=0
        ),
    )(short_filter)


def short_kernel(prior_ref, own_ref, gate_ref, band_ref, mid_ref):
    groups = band_ref.shape[0]
    channels = own_ref.shape[1]
    size = channels // groups
    for b in range(channels // LANES):
        cols = slice(b * LANES, (b + 1) * LANES)
        prior = prior_ref[:, cols].astype(F32).T.astype(BF16)
        own = own_ref[:, cols].astype(F32).T.astype(BF16)
        gate = gate_ref[:, cols].astype(F32).T
        both = jnp.concatenate([prior, own], axis=1)
        for s in range(LANES // size):
            rows = slice(s * size, (s + 1) * size)
            out = jnp.dot(
                both[rows, :], band_ref[b * (LANES // size) + s], preferred_element_type=F32
            )
            start = b * LANES + s * size
            mid_ref[start : start + size, :] = (gate[rows, :] * out).astype(BF16)


def short_stage(prior, own, gate, band):
    tokens, channels = own.shape
    return pl.pallas_call(
        short_kernel,
        out_shape=jax.ShapeDtypeStruct((channels, tokens), BF16),
        name="short_stage",
        compiler_params=pltpu.CompilerParams(vmem_limit_bytes=16 << 20),
        cost_estimate=pl.CostEstimate(
            flops=1_000_000_000, bytes_accessed=4 << 20, transcendentals=0
        ),
    )(prior, own, gate, band)


def toeplitz_kernel(steps, filt_ref, out_ref, last):
    own = upper()
    q = pl.program_id(0)

    @pl.when(q == 0)
    def _():
        last[...] = jnp.zeros(last.shape, F32)

    for c in range(filt_ref.shape[0]):
        before = last[c]
        for j in range(steps):
            turned = rolled_rows(filt_ref[c : c + 1, j * LANES : (j + 1) * LANES])
            block = jnp.where(own, turned, before).astype(BF16)
            out_ref[c, j * LANES : (j + 1) * LANES, :] = block
            before = turned
        last[c] = before


def long_blocks(long_filter, steps):
    rows, seq = long_filter.shape
    deep, wide = steps * LANES, seq // steps
    return pl.pallas_call(
        lambda *refs: toeplitz_kernel(steps, *refs),
        grid=(wide // LANES,),
        in_specs=[pl.BlockSpec((rows, deep), lambda q: (0, q))],
        out_specs=pl.BlockSpec((rows, deep, LANES), lambda q: (0, 0, q)),
        out_shape=jax.ShapeDtypeStruct((rows, deep, wide), BF16),
        scratch_shapes=[pltpu.VMEM((rows, LANES, LANES), F32)],
        name="long_blocks",
        compiler_params=pltpu.CompilerParams(vmem_limit_bytes=12 << 20),
        cost_estimate=pl.CostEstimate(
            flops=8_000_000_000, bytes_accessed=rows * deep * wide * 2, transcendentals=0
        ),
    )(long_filter)


def conv_kernel(steps, sig_ref, blk_ref, out_ref, sig, acc):
    c = pl.program_id(0)
    count, rows = sig_ref.shape[0], sig_ref.shape[1]

    @pl.when(c == 0)
    def _():
        sig[...] = sig_ref[...].reshape(count * rows, LANES).astype(F32)

    u = sig[pl.ds(c, count, stride=rows), :]
    at = lax.broadcasted_iota(jnp.int32, (count, LANES), 0)
    shifted = [u.astype(BF16)]
    for j in range(1, steps):
        shifted.append(jnp.where(at >= j, pltpu.roll(u, j, axis=0), 0.0).astype(BF16))
    lhs = jnp.concatenate(shifted, axis=1)
    wide = blk_ref.shape[2]
    half = wide // 2
    near = jnp.dot(lhs, blk_ref[0, :, :half], preferred_element_type=F32)
    far = jnp.dot(lhs[: count // 2], blk_ref[0, :, half:], preferred_element_type=F32)
    total = near[:, :LANES]
    for q in range(1, wide // LANES):
        down = q * steps
        if q * LANES < half:
            part = near[: count - down, q * LANES : (q + 1) * LANES]
        else:
            part = far[: count - down, q * LANES - half : (q + 1) * LANES - half]
        total = total + jnp.concatenate([jnp.zeros((down, LANES), F32), part], axis=0)
    acc[pl.ds(c, count, stride=rows), :] = total

    @pl.when(c == rows - 1)
    def _():
        out_ref[...] = acc[...].reshape(count, rows, LANES).astype(BF16)


def long_stage(signal, blocks, steps):
    count, rows, _ = signal.shape
    _, deep, wide = blocks.shape
    return pl.pallas_call(
        lambda *refs: conv_kernel(steps, *refs),
        grid=(rows,),
        in_specs=[
            pl.BlockSpec((count, rows, LANES), lambda c: (0, 0, 0)),
            pl.BlockSpec((1, deep, wide), lambda c: (c, 0, 0)),
        ],
        out_specs=pl.BlockSpec((count, rows, LANES), lambda c: (0, 0, 0)),
        out_shape=jax.ShapeDtypeStruct(signal.shape, BF16),
        scratch_shapes=[
            pltpu.VMEM((count * rows, LANES), F32),
            pltpu.VMEM((count * rows, LANES), F32),
        ],
        name="long_stage",
        compiler_params=pltpu.CompilerParams(vmem_limit_bytes=16 << 20),
        cost_estimate=pl.CostEstimate(
            flops=8_000_000_000, bytes_accessed=rows * deep * wide * 2, transcendentals=0
        ),
    )(signal, blocks)


def gate_kernel(far, near, long_ref, mid_ref, gate_ref, skip_ref, out_ref):
    channels = gate_ref.shape[1]
    tiles = []
    for b in range(channels // LANES):
        rows = slice(b * LANES, (b + 1) * LANES)
        whole = long_ref[rows, :].astype(F32).T
        mid = mid_ref[rows, :].astype(F32).T
        gate = gate_ref[:, rows].astype(F32)
        tiles.append(gate * (whole + skip_ref[:, rows] * mid))
    half = LANES // 2
    low = lax.broadcasted_iota(jnp.int32, tiles[0].shape, 1) < half

    def piece(i, upper_half):
        tile = tiles[i // 2]
        return tile if (i % 2 == 1) == upper_half else pltpu.roll(tile, half, axis=1)

    for y in range(near):
        both = jnp.where(low, piece(y, False), piece(near + y, True)).astype(BF16)
        for copy in range(out_ref.shape[0]):
            out_ref[copy, :, y * LANES : (y + 1) * LANES] = both


def gate_stage(long_rows, mid_rows, gate, skip, copies, near):
    tokens, channels = gate.shape
    return pl.pallas_call(
        lambda *refs: gate_kernel(2, near, *refs),
        out_shape=jax.ShapeDtypeStruct((copies, tokens, channels), BF16),
        name="gate_stage",
        compiler_params=pltpu.CompilerParams(vmem_limit_bytes=16 << 20),
        cost_estimate=pl.CostEstimate(
            flops=1_000_000_000, bytes_accessed=1 << 20, transcendentals=0
        ),
    )(long_rows, mid_rows, gate, skip)


def project_kernel(near, own_ref, other_ref, weight_ref, out_ref, acc):
    k = pl.program_id(0)
    even = lax.axis_index("core") == 0
    total = jnp.zeros(acc.shape, F32)
    own, other = own_ref[0], other_ref[0]
    first = jnp.where(even, own, other)
    second = jnp.where(even, other, own)
    for y in range(near):
        cols = slice(y * LANES, (y + 1) * LANES)
        lhs = jnp.concatenate([first[:, cols], second[:, cols]], axis=1)
        total += jnp.dot(
            lhs, weight_ref[y * 2 * LANES : (y + 1) * 2 * LANES, :], preferred_element_type=F32
        )

    @pl.when(k == 0)
    def _():
        acc[...] = total

    @pl.when(k > 0)
    def _():
        acc[...] += total

    @pl.when(k == pl.num_programs(0) - 1)
    def _():
        out_ref[...] = acc[...].astype(BF16)


def project(own, other, weight, near):
    blocks, tokens, channels = own.shape
    cols = weight.shape[1]
    return pl.pallas_call(
        lambda *refs: project_kernel(near, *refs),
        grid=(blocks,),
        in_specs=[
            pl.BlockSpec((1, tokens, channels), lambda k: (k, 0, 0)),
            pl.BlockSpec((1, tokens, channels), lambda k: (k, 0, 0)),
            pl.BlockSpec((2 * channels, cols), lambda k: (k, 0)),
        ],
        out_specs=pl.BlockSpec((tokens, cols), lambda k: (0, 0)),
        out_shape=jax.ShapeDtypeStruct((tokens, cols), BF16),
        scratch_shapes=[pltpu.VMEM((tokens, cols), F32)],
        name="project",
        compiler_params=pltpu.CompilerParams(vmem_limit_bytes=16 << 20),
    )(own, other, weight)


def next_tokens(value):
    size = lax.axis_size(CTX)
    return lax.ppermute(value, CTX, [(s, s + 1) for s in range(size - 1)])


def in_hbm(value):
    return pltpu.with_memory_space_constraint(value, pltpu.HBM)


def to_each(parts, axes):
    return lax.all_to_all(parts, axes, 0, 0, tiled=True)


def shards(
    value_in, key_in, gate_short, gate_long, short_filter, long_filter, skip_gain, out_weight
):
    tokens, channels = value_in.shape
    ways = lax.axis_size(CTX)
    per_dev = channels // ways
    steps = 8

    product = (value_in.astype(F32) * key_in.astype(F32)).astype(BF16)
    prior = next_tokens(product)
    copies = jnp.broadcast_to(out_weight[None], (lax.axis_size("zh"), *out_weight.shape))
    weight_rows = to_each(copies, "zh").reshape(-1, out_weight.shape[1])
    weight = in_hbm(lax.all_gather(weight_rows, ("x", "y"), axis=0, tiled=True))

    mid = short_stage(prior, product, gate_short, short_bands(short_filter))
    spread = to_each(mid.reshape(ways, per_dev, tokens), CTX)
    blocks = in_hbm(long_blocks(long_filter, steps))
    long_part = long_stage(spread, blocks, steps)
    returned = to_each(long_part, CTX).reshape(channels, tokens)
    near = lax.axis_size("y")
    gated = gate_stage(
        returned, mid, gate_long, skip_gain[None, :], lax.axis_size("zl"), near
    )
    own = to_each(gated, "zl")
    other = lax.ppermute(own, "core", [(0, 1), (1, 0)])
    return project(own, other, weight, near)


def solution(mesh):
    fine = Mesh(mesh.devices.reshape(4, 4, 4, 4, 2), CTX + CH)
    in_specs = (
        P(CTX, CH),
        P(CTX, CH),
        P(CTX, CH),
        P(CTX, CH),
        P(CH, None),
        P(CH + CTX, None),
        P(CH),
        P(CTX, CH),
    )
    return jax.shard_map(
        shards, mesh=fine, in_specs=in_specs, out_specs=P(CTX, CH), check_vma=False
    )
```

time: 189 us -> 163 us (0.86)
  waiting for transfers between devices: 47.5 us -> 2.59 us
  blocking collectives: 47.6 us -> 85.5 us
  Pallas kernels: 0 us -> 26.5 us
  matrix products: 24.4 us -> 0 us
  local copies, waits for them, and re-layouts: 17 us -> 7.3 us
  starting transfers between devices: 34.9 us -> 26.1 us
  other arithmetic: 3.34 us -> 1 us
    all_to_all x3 -> x1, waiting for transfers between devices: 47.4 us -> 0.19 us  [to_each(): return lax.all_to_all(parts, axes, 0, 0, tiled=True)]
    all_to_all x1 -> x3, blocking collectives: 47.6 us -> 85.5 us  [to_each(): return lax.all_to_all(parts, axes, 0, 0, tiled=True)]
    pallas_call x0 -> x6, Pallas kernels: none -> 26.5 us  [the longest x1 10.3 us: long_blocks(): pl.pallas_call(lambda *refs: toeplitz_kernel(steps, *refs), grid=(wide //...]
    dot_general x20 -> x0, matrix products: 24.4 us -> none  [the longest x12 13.3 us: right_mul(): jnp.einsum('ckn,nq->ckq', signal, matrix, precision=lax.Precision.HIGHEST)]
    all_to_all x3 -> x1, starting transfers between devices: 30.9 us -> 16.5 us  [to_each(): return lax.all_to_all(parts, axes, 0, 0, tiled=True)]
    reshape x2 -> x0, local copies, waits for them, and re-layouts: 9.37 us -> none  [the longest x1 9.26 us: toeplitz(): jnp.tile(band_line, (1, width))[:, :width * row_span]]
    ppermute x1 -> x2, starting transfers between devices: 4.03 us -> 9.64 us  [the longest x1 6.3 us: shards(): other = lax.ppermute(own, 'core', [(0, 1), (1, 0)])]
    unnamed x16 -> x12, local copies, waits for them, and re-layouts: 3.34 us -> 6.44 us
  transfers between devices with their start and end apart: 5 -> 4, of which waited for: 3 -> 3; matrix products, arithmetic and copies ran while one was open for 21% -> 1% of each run, Pallas kernels for 0% -> 14%
where the time goes in v1:
time: 163 us; the launch traced here: 162 us
  blocking collectives  85.5 us (52%)
  Pallas kernels  26.5 us (16%)
  starting transfers between devices  26.1 us (16%)
  between operations  13.5 us (8%)
  local copies, waits for them, and re-layouts  7.3 us (4%)
  waiting for transfers between devices  2.59 us (2%)
    all_to_all x3, blocking collectives, to_each(): return lax.all_to_all(parts, axes, 0, 0, tiled=True)  85.5 us
    all_to_all x1, starting transfers between devices, to_each(): return lax.all_to_all(parts, axes, 0, 0, tiled=True)  16.5 us
    pallas_call x1, Pallas kernels, long_blocks(): pl.pallas_call(lambda *refs: toeplitz_kernel(steps, *refs), grid=(wide //...  10.3 us
    pallas_call x1, Pallas kernels, long_stage(): pl.pallas_call(lambda *refs: conv_kernel(steps, *refs), grid=(rows,), in_...  9.4 us
    unnamed x12, local copies, waits for them, and re-layouts  6.44 us
    ppermute x1, starting transfers between devices, shards(): other = lax.ppermute(own, 'core', [(0, 1), (1, 0)])  6.3 us
    pallas_call x1, Pallas kernels, project(): pl.pallas_call(lambda *refs: project_kernel(near, *refs), grid=(blocks,),...  4.2 us
    ppermute x1, starting transfers between devices, next_tokens(): return lax.ppermute(value, CTX, [(s, s + 1) for s in range(size - 1)])  3.34 us
  transfers between devices with their start and end apart: 4, of which 3 were waited for; matrix products, arithmetic and copies ran while one was open for 1% of the time, Pallas kernels for 14%

profile of v1, /device:TPU:1, one launch (start us, length us, event | category | flops | bytes accessed | tf_op | source)
XLA Modules:
  0.0 162.4 jit_solution(9163846643100724130)
XLA Ops:
  6.5 0.0 all-gather.2.cloned.1.call-start
  6.5 0.9 broadcast_in_dim.10
  7.4 0.0 copy-start.1
  7.4 29.9 %all_to_all.20 = bf16[4,64,512]{2,1,0:T(8,128)(2,1)} all-to-all(bf16[4,64,512]{2,1,0:T(8,128)(2,1)S(1)} %broadcast_in_dim.10), channel_id=1, replica_groups=mesh['x'=4,'zh'=4,'y'=4,'zl'=4,'core'=2] {'zh'}, dimensions={0} | all-to-all | bytes 524288 | tf_op jit(solution)/shard_map/all_to_all | solution.py:265
  37.3 0.0 all-gather.2.cloned.1.call-update
  37.3 1.0 multiply_convert_fusion.own_ref
  38.3 0.0 copy-start
  38.3 3.3 %collective-permute-start = (bf16[128,512]{1,0:T(8,128)(2,1)S(1)}, bf16[128,512]{1,0:T(8,128)(2,1)S(1)}, u32[]{:S(2)}, u32[]{:S(2)}) collective-permute-start(bf16[128,512]{1,0:T(8,128)(2,1)S(1)} %multiply_convert_fusion.own_ref), channel_id=1, source_target_pairs={{0,8},{8,16},{16,24},{24,32},{32,40},{40,48},{48,56},{56,64},{64,7... | collective-permute-start | bytes 393224 | tf_op jit(solution)/shard_map/ppermute | solution.py:257
  41.7 0.0 copy-start.3
  41.7 0.7 copy-done.3
  42.4 0.4 short_bands.1.band_ref
  42.7 0.9 collective-permute-done.prior_ref
  43.6 0.0 copy-done.1
  43.6 1.1 short_stage.1.refs_1_
  44.7 16.5 %all-to-all-start = ((bf16[64,8,128]{2,1,0:T(8,128)(2,1)}), bf16[64,8,128]{2,1,0:T(8,128)(2,1)S(1)}, u32[]{:S(2)}, u32[]{:S(2)}) async-start(bf16[64,8,128]{2,1,0:T(8,128)(2,1)} %bitcast), calls=%async_computation | async-start | bytes 262144 | tf_op jit(solution)/shard_map/all_to_all | solution.py:265
  61.2 0.0 copy-done
  61.2 10.3 %long_blocks.1.refs_1_ = bf16[8,1024,1024]{2,1,0:T(8,128)(2,1)S(1)} custom-call(f32[8,8192]{1,0:T(8,128)S(1)} %copy-done), custom_call_target="tpu_custom_call" | custom-call | flops 8000000000 | bytes 16777216 | tf_op jit(solution)/shard_map/long_blocks/pallas_call | solution.py:102
  71.5 0.0 copy-start.5
  71.5 5.7 %copy-done.5 = bf16[8,1024,1024]{2,1,0:T(8,128)(2,1)} copy-done((bf16[8,1024,1024]{2,1,0:T(8,128)(2,1)}, bf16[8,1024,1024]{2,1,0:T(8,128)(2,1)S(1)}, u32[]{:S(2)}) %copy-start.5) | copy-done | bytes 16777240
  77.2 0.0 copy-start.2
  77.2 0.0 copy-start.4
  77.2 0.2 all-to-all-done.refs_0_
  77.4 9.4 %long_stage.1 = bf16[64,8,128]{2,1,0:T(8,128)(2,1)S(1)} custom-call(bf16[64,8,128]{2,1,0:T(8,128)(2,1)S(1)} %all-to-all-done.refs_0_, bf16[8,1024,1024]{2,1,0:T(8,128)(2,1)} %copy-done.5), custom_call_target="tpu_custom_call" | custom-call | flops 8000000000 | bytes 16777216 | tf_op jit(solution)/shard_map/long_stage/pallas_call | solution.py:153
  86.8 33.2 %all_to_all.21 = bf16[64,8,128]{2,1,0:T(8,128)(2,1)S(1)} all-to-all(bf16[64,8,128]{2,1,0:T(8,128)(2,1)S(1)} %long_stage.1), channel_id=1, replica_groups=mesh['x'=4,'zh'=4,'y'=4,'zl'=4,'core'=2] {'x','zh','y'}, dimensions={0} | all-to-all | bytes 262144 | tf_op jit(solution)/shard_map/all_to_all | solution.py:265
  120.0 0.0 copy-done.2
  120.0 0.0 copy-done.4
  120.0 1.2 gate_stage.1
  121.2 22.4 %all_to_all.22.refs_0_ = bf16[4,128,512]{2,1,0:T(8,128)(2,1)S(1)} all-to-all(bf16[4,128,512]{2,1,0:T(8,128)(2,1)S(1)} %gate_stage.1), channel_id=1, replica_groups=mesh['x'=4,'zh'=4,'y'=4,'zl'=4,'core'=2] {'zl'}, dimensions={0} | all-to-all | bytes 1048576 | tf_op jit(solution)/shard_map/all_to_all | solution.py:265
  143.6 6.3 %collective-permute-start.1 = (bf16[4,128,512]{2,1,0:T(8,128)(2,1)S(1)}, bf16[4,128,512]{2,1,0:T(8,128)(2,1)S(1)}, u32[]{:S(2)}, u32[]{:S(2)}) collective-permute-start(bf16[4,128,512]{2,1,0:T(8,128)(2,1)S(1)} %all_to_all.22.refs_0_), channel_id=1, source_target_pairs={{0,1},{1,0},{2,3},{3,2},{4,5},{5,4},{6,7},{7,6},{8,9},{9,8},{10,11... | collective-permute-start | bytes 1572872 | tf_op jit(solution)/shard_map/ppermute | solution.py:292
  149.9 1.5 collective-permute-done.1.refs_1_
  151.4 0.0 all-gather.2.cloned.1.call-done.refs_2_
  151.4 4.2 %project.1 = bf16[128,512]{1,0:T(8,128)(2,1)} custom-call(bf16[4,128,512]{2,1,0:T(8,128)(2,1)S(1)} %all_to_all.22.refs_0_, bf16[4,128,512]{2,1,0:T(8,128)(2,1)S(1)} %collective-permute-done.1.refs_1_, bf16[4096,512]{1,0:T(8,128)(2,1)} %all-gather.2.cloned.1.call-done.refs_2_), custom_call_target="tpu_custom_call" | custom-call | tf_op jit(solution)/shard_map/project/pallas_call | solution.py:239
Async XLA Ops:
  6.5 144.9 %all-gather.2.cloned.1.call-start = ((), (), s32[]{:S(2)}) async-start(), calls=%async_computation.4 | async-start | bytes 4456448 | tf_op jit(solution)/shard_map/all_gather | solution.py:280
  7.4 36.2 %copy-start.1 = (bf16[128,512]{1,0:T(8,128)(2,1)S(1)}, bf16[128,512]{1,0:T(8,128)(2,1)}, u32[]{:S(2)}) copy-start(bf16[128,512]{1,0:T(8,128)(2,1)} %gate_ref.1) | copy-start | bytes 393220
  38.3 22.9 %copy-start = (f32[8,8192]{1,0:T(8,128)S(1)}, f32[8,8192]{1,0:T(8,128)}, u32[]{:S(2)}) copy-start(f32[8,8192]{1,0:T(8,128)} %refs_0_.1) | copy-start | bytes 786436
  38.3 5.3 %collective-permute-start = (bf16[128,512]{1,0:T(8,128)(2,1)S(1)}, bf16[128,512]{1,0:T(8,128)(2,1)S(1)}, u32[]{:S(2)}, u32[]{:S(2)}) collective-permute-start(bf16[128,512]{1,0:T(8,128)(2,1)S(1)} %multiply_convert_fusion.own_ref), channel_id=1, source_target_pairs={{0,8},{8,16},{16,24},{24,32},{32,40},{40,48},{48,56},{56,64},{64,7... | collective-permute-start | bytes 393224 | tf_op jit(solution)/shard_map/ppermute | solution.py:257
  41.7 0.7 copy-start.3
  44.7 32.7 %all-to-all-start = ((bf16[64,8,128]{2,1,0:T(8,128)(2,1)}), bf16[64,8,128]{2,1,0:T(8,128)(2,1)S(1)}, u32[]{:S(2)}, u32[]{:S(2)}) async-start(bf16[64,8,128]{2,1,0:T(8,128)(2,1)} %bitcast), calls=%async_computation | async-start | bytes 262144 | tf_op jit(solution)/shard_map/all_to_all | solution.py:265
  71.5 5.7 %copy-start.5 = (bf16[8,1024,1024]{2,1,0:T(8,128)(2,1)}, bf16[8,1024,1024]{2,1,0:T(8,128)(2,1)S(1)}, u32[]{:S(2)}) copy-start(bf16[8,1024,1024]{2,1,0:T(8,128)(2,1)S(1)} %long_blocks.1.refs_1_) | copy-start | bytes 50331652
  77.2 42.8 %copy-start.2 = (bf16[128,512]{1,0:T(8,128)(2,1)S(1)}, bf16[128,512]{1,0:T(8,128)(2,1)}, u32[]{:S(2)}) copy-start(bf16[128,512]{1,0:T(8,128)(2,1)} %refs_2_.1) | copy-start | bytes 393220
  77.2 42.8 %copy-start.4 = (f32[512]{0:T(512)S(1)}, f32[512]{0:T(512)}, u32[]{:S(2)}) copy-start(f32[512]{0:T(512)} %param.14) | copy-start | bytes 6148
  143.6 7.8 %collective-permute-start.1 = (bf16[4,128,512]{2,1,0:T(8,128)(2,1)S(1)}, bf16[4,128,512]{2,1,0:T(8,128)(2,1)S(1)}, u32[]{:S(2)}, u32[]{:S(2)}) collective-permute-start(bf16[4,128,512]{2,1,0:T(8,128)(2,1)S(1)} %all_to_all.22.refs_0_), channel_id=1, source_target_pairs={{0,1},{1,0},{2,3},{3,2},{4,5},{5,4},{6,7},{7,6},{8,9},{9,8},{10,11... | collective-permute-start | bytes 1572872 | tf_op jit(solution)/shard_map/ppermute | solution.py:292
Sparse Core Ops, SparseCore 0:
  37.4 66.8 all-gather.1

commit v2 on v1

--- a/solution.py
+++ b/solution.py
@@ -9,19 +9,20 @@
 CTX = ("x", "zh", "y")
 CH = ("zl", "core")
 LANES = 128
+HALF = LANES // 2
 F32 = jnp.float32
 BF16 = jnp.bfloat16
 
 
-def rolled_rows(row):
-    square = jnp.broadcast_to(row, (LANES, LANES))
+def rolled_rows(row, rows=LANES):
+    square = jnp.broadcast_to(row, (rows, LANES))
     return pltpu.roll(square, 0, axis=1, stride=1, stride_axis=0)
 
 
-def upper():
-    rows = lax.broadcasted_iota(jnp.int32, (LANES, LANES), 0)
-    cols = lax.broadcasted_iota(jnp.int32, (LANES, LANES), 1)
-    return cols >= rows
+def upper(rows=LANES):
+    at = lax.broadcasted_iota(jnp.int32, (rows, LANES), 0)
+    cols = lax.broadcasted_iota(jnp.int32, (rows, LANES), 1)
+    return cols >= at
 
 
 def band_kernel(taps_ref, band_ref):
@@ -78,84 +79,109 @@
     )(prior, own, gate, band)
 
 
-def toeplitz_kernel(steps, filt_ref, out_ref, last):
-    own = upper()
-    q = pl.program_id(0)
-
-    @pl.when(q == 0)
+def toeplitz_kernel(filt_ref, out_ref, last):
+    own = upper(HALF)
+
+    @pl.when(pl.program_id(0) == 0)
     def _():
         last[...] = jnp.zeros(last.shape, F32)
 
     for c in range(filt_ref.shape[0]):
         before = last[c]
-        for j in range(steps):
-            turned = rolled_rows(filt_ref[c : c + 1, j * LANES : (j + 1) * LANES])
-            block = jnp.where(own, turned, before).astype(BF16)
-            out_ref[c, j * LANES : (j + 1) * LANES, :] = block
+        for i in range(filt_ref.shape[1] // LANES):
+            cols = slice(i * LANES, (i + 1) * LANES)
+            turned = rolled_rows(filt_ref[c : c + 1, cols], HALF)
+            out_ref[c, :, cols] = jnp.where(own, turned, before).astype(BF16)
             before = turned
         last[c] = before
 
 
-def long_blocks(long_filter, steps):
+def long_blocks(long_filter):
     rows, seq = long_filter.shape
-    deep, wide = steps * LANES, seq // steps
-    return pl.pallas_call(
-        lambda *refs: toeplitz_kernel(steps, *refs),
-        grid=(wide // LANES,),
-        in_specs=[pl.BlockSpec((rows, deep), lambda q: (0, q))],
-        out_specs=pl.BlockSpec((rows, deep, LANES), lambda q: (0, 0, q)),
-        out_shape=jax.ShapeDtypeStruct((rows, deep, wide), BF16),
-        scratch_shapes=[pltpu.VMEM((rows, LANES, LANES), F32)],
+    steps = 8
+    wide = seq // steps
+    return pl.pallas_call(
+        toeplitz_kernel,
+        grid=(steps,),
+        in_specs=[pl.BlockSpec((rows, wide), lambda j: (0, j))],
+        out_specs=pl.BlockSpec((rows, HALF, wide), lambda j: (0, j, 0)),
+        out_shape=jax.ShapeDtypeStruct((rows, steps * HALF, wide), BF16),
+        scratch_shapes=[pltpu.VMEM((rows, HALF, LANES), F32)],
         name="long_blocks",
-        compiler_params=pltpu.CompilerParams(vmem_limit_bytes=12 << 20),
-        cost_estimate=pl.CostEstimate(
-            flops=8_000_000_000, bytes_accessed=rows * deep * wide * 2, transcendentals=0
+        compiler_params=pltpu.CompilerParams(vmem_limit_bytes=58 << 20),
+        cost_estimate=pl.CostEstimate(
+            flops=4_000_000_000, bytes_accessed=rows * steps * HALF * wide * 2, transcendentals=0
         ),
     )(long_filter)
 
 
-def conv_kernel(steps, sig_ref, blk_ref, out_ref, sig, acc):
-    c = pl.program_id(0)
+def moved_down(x, rows):
+    if rows == 0:
+        return x
+    return jnp.concatenate([jnp.zeros((rows, x.shape[1]), x.dtype), x[:-rows]], axis=0)
+
+
+def turned_down(x, rows, at):
+    return x if rows == 0 else jnp.where(at >= rows, pltpu.roll(x, rows, axis=0), 0.0)
+
+
+def conv_channel(u, blk_ref, i):
+    count = u.shape[0]
+    at = lax.broadcasted_iota(jnp.int32, u.shape, 0)
+    low = lax.broadcasted_iota(jnp.int32, u.shape, 1) < HALF
+    w = pltpu.roll(u, HALF, axis=1)
+    deep, wide = blk_ref.shape[1:]
+    per = wide // (2 * HALF)
+    halves = []
+    for first, second in ((u, w), (w, u)):
+        tiles = [
+            jnp.where(low, moved_down(first, per * j), moved_down(second, per * (j + 1)))
+            for j in range(0, deep // HALF, 2)
+        ]
+        halves.append(jnp.concatenate(tiles, axis=1))
+    lhs = jnp.concatenate(halves, axis=0).astype(BF16)
+    even = jnp.zeros(u.shape, F32)
+    odd = jnp.zeros(u.shape, F32)
+    for p in range(0, per, 2):
+        both = jnp.dot(
+            lhs, blk_ref[i, :, p * LANES : (p + 2) * LANES], preferred_element_type=F32
+        )
+        for k in range(2):
+            part = both[:, k * LANES : (k + 1) * LANES]
+            even += turned_down(part[:count], p + k, at)
+            odd += turned_down(part[count:], p + k, at)
+    odd = pltpu.roll(odd, HALF, axis=1)
+    return even + jnp.where(low, turned_down(odd, 1, at), odd)
+
+
+def conv_kernel(sig_ref, blk_ref, out_ref, sig, acc):
+    step = pl.program_id(0)
     count, rows = sig_ref.shape[0], sig_ref.shape[1]
-
-    @pl.when(c == 0)
+    each = blk_ref.shape[0]
+
+    @pl.when(step == 0)
     def _():
         sig[...] = sig_ref[...].reshape(count * rows, LANES).astype(F32)
 
-    u = sig[pl.ds(c, count, stride=rows), :]
-    at = lax.broadcasted_iota(jnp.int32, (count, LANES), 0)
-    shifted = [u.astype(BF16)]
-    for j in range(1, steps):
-        shifted.append(jnp.where(at >= j, pltpu.roll(u, j, axis=0), 0.0).astype(BF16))
-    lhs = jnp.concatenate(shifted, axis=1)
-    wide = blk_ref.shape[2]
-    half = wide // 2
-    near = jnp.dot(lhs, blk_ref[0, :, :half], preferred_element_type=F32)
-    far = jnp.dot(lhs[: count // 2], blk_ref[0, :, half:], preferred_element_type=F32)
-    total = near[:, :LANES]
-    for q in range(1, wide // LANES):
-        down = q * steps
-        if q * LANES < half:
-            part = near[: count - down, q * LANES : (q + 1) * LANES]
-        else:
-            part = far[: count - down, q * LANES - half : (q + 1) * LANES - half]
-        total = total + jnp.concatenate([jnp.zeros((down, LANES), F32), part], axis=0)
-    acc[pl.ds(c, count, stride=rows), :] = total
-
-    @pl.when(c == rows - 1)
+    for i in range(each):
+        at = pl.ds(step * each + i, count, stride=rows)
+        acc[at, :] = conv_channel(sig[at, :], blk_ref, i)
+
+    @pl.when(step == pl.num_programs(0) - 1)
     def _():
         out_ref[...] = acc[...].reshape(count, rows, LANES).astype(BF16)
 
 
-def long_stage(signal, blocks, steps):
+def long_stage(signal, blocks):
     count, rows, _ = signal.shape
     _, deep, wide = blocks.shape
-    return pl.pallas_call(
-        lambda *refs: conv_kernel(steps, *refs),
-        grid=(rows,),
+    each = 2
+    return pl.pallas_call(
+        conv_kernel,
+        grid=(rows // each,),
         in_specs=[
             pl.BlockSpec((count, rows, LANES), lambda c: (0, 0, 0)),
-            pl.BlockSpec((1, deep, wide), lambda c: (c, 0, 0)),
+            pl.BlockSpec((each, deep, wide), lambda c: (c, 0, 0)),
         ],
         out_specs=pl.BlockSpec((count, rows, LANES), lambda c: (0, 0, 0)),
         out_shape=jax.ShapeDtypeStruct(signal.shape, BF16),
@@ -171,7 +197,7 @@
     )(signal, blocks)
 
 
-def gate_kernel(far, near, long_ref, mid_ref, gate_ref, skip_ref, out_ref):
+def gate_kernel(near, long_ref, mid_ref, gate_ref, skip_ref, out_ref):
     channels = gate_ref.shape[1]
     tiles = []
     for b in range(channels // LANES):
@@ -196,7 +222,7 @@
 def gate_stage(long_rows, mid_rows, gate, skip, copies, near):
     tokens, channels = gate.shape
     return pl.pallas_call(
-        lambda *refs: gate_kernel(2, near, *refs),
+        lambda *refs: gate_kernel(near, *refs),
         out_shape=jax.ShapeDtypeStruct((copies, tokens, channels), BF16),
         name="gate_stage",
         compiler_params=pltpu.CompilerParams(vmem_limit_bytes=16 << 20),
@@ -271,23 +297,20 @@
     tokens, channels = value_in.shape
     ways = lax.axis_size(CTX)
     per_dev = channels // ways
-    steps = 8
-
-    product = (value_in.astype(F32) * key_in.astype(F32)).astype(BF16)
-    prior = next_tokens(product)
+    near = lax.axis_size("y")
+
     copies = jnp.broadcast_to(out_weight[None], (lax.axis_size("zh"), *out_weight.shape))
     weight_rows = to_each(copies, "zh").reshape(-1, out_weight.shape[1])
     weight = in_hbm(lax.all_gather(weight_rows, ("x", "y"), axis=0, tiled=True))
-
-    mid = short_stage(prior, product, gate_short, short_bands(short_filter))
+    product = (value_in.astype(F32) * key_in.astype(F32)).astype(BF16)
+    prior = next_tokens(product)
+    bands = short_bands(short_filter)
+    mid = short_stage(prior, product, gate_short, bands)
     spread = to_each(mid.reshape(ways, per_dev, tokens), CTX)
-    blocks = in_hbm(long_blocks(long_filter, steps))
-    long_part = long_stage(spread, blocks, steps)
+    blocks = in_hbm(long_blocks(long_filter))
+    long_part = long_stage(spread, blocks)
     returned = to_each(long_part, CTX).reshape(channels, tokens)
-    near = lax.axis_size("y")
-    gated = gate_stage(
-        returned, mid, gate_long, skip_gain[None, :], lax.axis_size("zl"), near
-    )
+    gated = gate_stage(returned, mid, gate_long, skip_gain[None, :], lax.axis_size("zl"), near)
     own = to_each(gated, "zl")
     other = lax.ppermute(own, "core", [(0, 1), (1, 0)])
     return project(own, other, weight, near)

time: 163 us -> 150 us (0.920)
  blocking collectives: 85.5 us -> 76.2 us
  waiting for transfers between devices: 2.59 us -> 11.6 us
  Pallas kernels: 26.5 us -> 19 us
  local copies, waits for them, and re-layouts: 7.3 us -> 1.56 us
    all_to_all x3, blocking collectives: 85.5 us -> 76.2 us  [to_each(): return lax.all_to_all(parts, axes, 0, 0, tiled=True)]
    all_to_all x1, waiting for transfers between devices: 0.19 us -> 9.16 us  [to_each(): return lax.all_to_all(parts, axes, 0, 0, tiled=True)]
    pallas_call x3, Pallas kernels: 20.8 us -> 13.4 us  [the longest x1 7.06 us: long_blocks(): pl.pallas_call(toeplitz_kernel, grid=(steps,), in_specs=[pl.BlockSpec((ro...]
    unnamed x12 -> x8, local copies, waits for them, and re-layouts: 6.44 us -> 0.71 us
  transfers between devices with their start and end apart: 4 -> 4, of which waited for: 3 -> 3; matrix products, arithmetic and copies ran while one was open for 1% -> 1% of each run, Pallas kernels for 14% -> 10%
where the time goes in v2:
time: 150 us; the launch traced here: 149 us
  blocking collectives  76.2 us (51%)
  starting transfers between devices  25.9 us (17%)
  Pallas kernels  19 us (13%)
  between operations  13.5 us (9%)
  waiting for transfers between devices  11.6 us (8%)
  local copies, waits for them, and re-layouts  1.56 us (1%)
    all_to_all x3, blocking collectives, to_each(): return lax.all_to_all(parts, axes, 0, 0, tiled=True)  76.2 us
    all_to_all x1, starting transfers between devices, to_each(): return lax.all_to_all(parts, axes, 0, 0, tiled=True)  16.5 us
    all_to_all x1, waiting for transfers between devices, to_each(): return lax.all_to_all(parts, axes, 0, 0, tiled=True)  9.16 us
    pallas_call x1, Pallas kernels, long_blocks(): pl.pallas_call(toeplitz_kernel, grid=(steps,), in_specs=[pl.BlockSpec((ro...  7.06 us
    ppermute x1, starting transfers between devices, shards(): other = lax.ppermute(own, 'core', [(0, 1), (1, 0)])  6.24 us
    pallas_call x1, Pallas kernels, long_stage(): pl.pallas_call(conv_kernel, grid=(rows // each,), in_specs=[pl.BlockSpec(...  5.16 us
    pallas_call x1, Pallas kernels, project(): pl.pallas_call(lambda *refs: project_kernel(near, *refs), grid=(blocks,),...  4.21 us
    ppermute x1, starting transfers between devices, next_tokens(): return lax.ppermute(value, CTX, [(s, s + 1) for s in range(size - 1)])  3.21 us
  transfers between devices with their start and end apart: 4, of which 3 were waited for; matrix products, arithmetic and copies ran while one was open for 1% of the time, Pallas kernels for 10%

profile of v2, /device:TPU:1, one launch (start us, length us, event | category | flops | bytes accessed | tf_op | source)
XLA Modules:
  0.0 148.8 jit_solution(12355635187945290668)
XLA Ops:
  6.5 0.0 all-gather.2.cloned.1.call-start
  6.5 0.9 broadcast_in_dim.10
  7.4 0.0 copy-start
  7.4 29.9 %all_to_all.20 = bf16[4,64,512]{2,1,0:T(8,128)(2,1)} all-to-all(bf16[4,64,512]{2,1,0:T(8,128)(2,1)S(1)} %broadcast_in_dim.10), channel_id=1, replica_groups=mesh['x'=4,'zh'=4,'y'=4,'zl'=4,'core'=2] {'zh'}, dimensions={0} | all-to-all | bytes 524288 | tf_op jit(solution)/shard_map/all_to_all | solution.py:291
  37.3 0.0 all-gather.2.cloned.1.call-update
  37.3 1.0 multiply_convert_fusion.own_ref
  38.3 3.2 %collective-permute-start = (bf16[128,512]{1,0:T(8,128)(2,1)S(1)}, bf16[128,512]{1,0:T(8,128)(2,1)S(1)}, u32[]{:S(2)}, u32[]{:S(2)}) collective-permute-start(bf16[128,512]{1,0:T(8,128)(2,1)S(1)} %multiply_convert_fusion.own_ref), channel_id=1, source_target_pairs={{0,8},{8,16},{16,24},{24,32},{32,40},{40,48},{48,56},{56,64},{64,7... | collective-permute-start | bytes 393224 | tf_op jit(solution)/shard_map/ppermute | solution.py:283
  41.5 0.0 copy-start.2
  41.5 0.7 copy-done.2
  42.2 0.4 short_bands.1.band_ref
  42.6 0.9 collective-permute-done.prior_ref
  43.4 0.0 copy-done
  43.4 1.1 short_stage.1.refs_1_
  44.6 16.5 %all-to-all-start = ((bf16[64,8,128]{2,1,0:T(8,128)(2,1)}), bf16[64,8,128]{2,1,0:T(8,128)(2,1)S(1)}, u32[]{:S(2)}, u32[]{:S(2)}) async-start(bf16[64,8,128]{2,1,0:T(8,128)(2,1)} %bitcast), calls=%async_computation | async-start | bytes 262144 | tf_op jit(solution)/shard_map/all_to_all | solution.py:291
  61.0 7.1 %long_blocks.1.blk_ref = bf16[8,512,1024]{2,1,0:T(8,128)(2,1)} custom-call(f32[8,8192]{1,0:T(8,128)} %filt_ref.1), custom_call_target="tpu_custom_call" | custom-call | flops 4000000000 | bytes 8388608 | tf_op jit(solution)/shard_map/long_blocks/pallas_call | solution.py:103
  68.1 0.0 copy-start.1
  68.1 0.0 copy-start.3
  68.1 9.2 %all-to-all-done.sig_ref = bf16[64,8,128]{2,1,0:T(8,128)(2,1)S(1)} async-done(((bf16[64,8,128]{2,1,0:T(8,128)(2,1)}), bf16[64,8,128]{2,1,0:T(8,128)(2,1)S(1)}, u32[]{:S(2)}, u32[]{:S(2)}) %all-to-all-start) | async-done | bytes 131104 | tf_op jit(solution)/shard_map/all_to_all | solution.py:291
  77.3 5.2 %long_stage.1 = bf16[64,8,128]{2,1,0:T(8,128)(2,1)S(1)} custom-call(bf16[64,8,128]{2,1,0:T(8,128)(2,1)S(1)} %all-to-all-done.sig_ref, bf16[8,512,1024]{2,1,0:T(8,128)(2,1)} %long_blocks.1.blk_ref), custom_call_target="tpu_custom_call" | custom-call | flops 8000000000 | bytes 8388608 | tf_op jit(solution)/shard_map/long_stage/pallas_call | solution.py:179
  82.4 23.9 %all_to_all.21 = bf16[64,8,128]{2,1,0:T(8,128)(2,1)S(1)} all-to-all(bf16[64,8,128]{2,1,0:T(8,128)(2,1)S(1)} %long_stage.1), channel_id=1, replica_groups=mesh['x'=4,'zh'=4,'y'=4,'zl'=4,'core'=2] {'x','zh','y'}, dimensions={0} | all-to-all | bytes 262144 | tf_op jit(solution)/shard_map/all_to_all | solution.py:291
  106.3 0.0 copy-done.1
  106.3 0.0 copy-done.3
  106.3 1.2 gate_stage.1
  107.5 22.4 %all_to_all.22.refs_0_ = bf16[4,128,512]{2,1,0:T(8,128)(2,1)S(1)} all-to-all(bf16[4,128,512]{2,1,0:T(8,128)(2,1)S(1)} %gate_stage.1), channel_id=1, replica_groups=mesh['x'=4,'zh'=4,'y'=4,'zl'=4,'core'=2] {'zl'}, dimensions={0} | all-to-all | bytes 1048576 | tf_op jit(solution)/shard_map/all_to_all | solution.py:291
  129.9 6.2 %collective-permute-start.1 = (bf16[4,128,512]{2,1,0:T(8,128)(2,1)S(1)}, bf16[4,128,512]{2,1,0:T(8,128)(2,1)S(1)}, u32[]{:S(2)}, u32[]{:S(2)}) collective-permute-start(bf16[4,128,512]{2,1,0:T(8,128)(2,1)S(1)} %all_to_all.22.refs_0_), channel_id=1, source_target_pairs={{0,1},{1,0},{2,3},{3,2},{4,5},{5,4},{6,7},{7,6},{8,9},{9,8},{10,11... | collective-permute-start | bytes 1572872 | tf_op jit(solution)/shard_map/ppermute | solution.py:315
  136.2 1.5 %collective-permute-done.1.refs_1_ = bf16[4,128,512]{2,1,0:T(8,128)(2,1)S(1)} collective-permute-done((bf16[4,128,512]{2,1,0:T(8,128)(2,1)S(1)}, bf16[4,128,512]{2,1,0:T(8,128)(2,1)S(1)}, u32[]{:S(2)}, u32[]{:S(2)}) %collective-permute-start.1) | collective-permute-done | bytes 524320 | tf_op jit(solution)/shard_map/ppermute | solution.py:315
  137.7 0.0 all-gather.2.cloned.1.call-done.refs_2_
  137.7 4.2 %project.1 = bf16[128,512]{1,0:T(8,128)(2,1)} custom-call(bf16[4,128,512]{2,1,0:T(8,128)(2,1)S(1)} %all_to_all.22.refs_0_, bf16[4,128,512]{2,1,0:T(8,128)(2,1)S(1)} %collective-permute-done.1.refs_1_, bf16[4096,512]{1,0:T(8,128)(2,1)} %all-gather.2.cloned.1.call-done.refs_2_), custom_call_target="tpu_custom_call" | custom-call | tf_op jit(solution)/shard_map/project/pallas_call | solution.py:265
Async XLA Ops:
  6.5 131.2 %all-gather.2.cloned.1.call-start = ((), (), s32[]{:S(2)}) async-start(), calls=%async_computation.4 | async-start | bytes 4456448 | tf_op jit(solution)/shard_map/all_gather | solution.py:304
  7.4 36.1 %copy-start = (bf16[128,512]{1,0:T(8,128)(2,1)S(1)}, bf16[128,512]{1,0:T(8,128)(2,1)}, u32[]{:S(2)}) copy-start(bf16[128,512]{1,0:T(8,128)(2,1)} %gate_ref.1) | copy-start | bytes 393220
  38.3 5.1 %collective-permute-start = (bf16[128,512]{1,0:T(8,128)(2,1)S(1)}, bf16[128,512]{1,0:T(8,128)(2,1)S(1)}, u32[]{:S(2)}, u32[]{:S(2)}) collective-permute-start(bf16[128,512]{1,0:T(8,128)(2,1)S(1)} %multiply_convert_fusion.own_ref), channel_id=1, source_target_pairs={{0,8},{8,16},{16,24},{24,32},{32,40},{40,48},{48,56},{56,64},{64,7... | collective-permute-start | bytes 393224 | tf_op jit(solution)/shard_map/ppermute | solution.py:283
  41.5 0.7 copy-start.2
  44.6 32.7 %all-to-all-start = ((bf16[64,8,128]{2,1,0:T(8,128)(2,1)}), bf16[64,8,128]{2,1,0:T(8,128)(2,1)S(1)}, u32[]{:S(2)}, u32[]{:S(2)}) async-start(bf16[64,8,128]{2,1,0:T(8,128)(2,1)} %bitcast), calls=%async_computation | async-start | bytes 262144 | tf_op jit(solution)/shard_map/all_to_all | solution.py:291
  68.1 38.2 %copy-start.1 = (bf16[128,512]{1,0:T(8,128)(2,1)S(1)}, bf16[128,512]{1,0:T(8,128)(2,1)}, u32[]{:S(2)}) copy-start(bf16[128,512]{1,0:T(8,128)(2,1)} %refs_2_.1) | copy-start | bytes 393220
  68.1 38.2 %copy-start.3 = (f32[512]{0:T(512)S(1)}, f32[512]{0:T(512)}, u32[]{:S(2)}) copy-start(f32[512]{0:T(512)} %param.14) | copy-start | bytes 6148
  129.9 7.8 %collective-permute-start.1 = (bf16[4,128,512]{2,1,0:T(8,128)(2,1)S(1)}, bf16[4,128,512]{2,1,0:T(8,128)(2,1)S(1)}, u32[]{:S(2)}, u32[]{:S(2)}) collective-permute-start(bf16[4,128,512]{2,1,0:T(8,128)(2,1)S(1)} %all_to_all.22.refs_0_), channel_id=1, source_target_pairs={{0,1},{1,0},{2,3},{3,2},{4,5},{5,4},{6,7},{7,6},{8,9},{9,8},{10,11... | collective-permute-start | bytes 1572872 | tf_op jit(solution)/shard_map/ppermute | solution.py:315
Sparse Core Ops, SparseCore 0:
  37.4 67.3 all-gather.1

commit v3 on v2

--- a/solution.py
+++ b/solution.py
@@ -232,50 +232,57 @@
     )(long_rows, mid_rows, gate, skip)
 
 
-def project_kernel(near, own_ref, other_ref, weight_ref, out_ref, acc):
+def project_kernel(core_ref, *refs):
+    feature_ref, weight_ref, before_ref, out_ref, acc = refs
     k = pl.program_id(0)
-    even = lax.axis_index("core") == 0
-    total = jnp.zeros(acc.shape, F32)
-    own, other = own_ref[0], other_ref[0]
-    first = jnp.where(even, own, other)
-    second = jnp.where(even, other, own)
-    for y in range(near):
-        cols = slice(y * LANES, (y + 1) * LANES)
-        lhs = jnp.concatenate([first[:, cols], second[:, cols]], axis=1)
-        total += jnp.dot(
-            lhs, weight_ref[y * 2 * LANES : (y + 1) * 2 * LANES, :], preferred_element_type=F32
-        )
+    rows = weight_ref.shape[1] * weight_ref.shape[3]
+    weight = weight_ref[...].reshape(rows, weight_ref.shape[4])
+    part = jnp.dot(feature_ref[0], weight, preferred_element_type=F32)
 
     @pl.when(k == 0)
     def _():
-        acc[...] = total
+        acc[...] = part if before_ref is None else before_ref[...] + part
 
     @pl.when(k > 0)
     def _():
-        acc[...] += total
+        acc[...] += part
 
     @pl.when(k == pl.num_programs(0) - 1)
     def _():
-        out_ref[...] = acc[...].astype(BF16)
-
-
-def project(own, other, weight, near):
-    blocks, tokens, channels = own.shape
+        out_ref[...] = acc[...].astype(out_ref.dtype)
+
+
+def project(features, weight, core, before, near):
+    blocks, tokens, channels = features.shape
     cols = weight.shape[1]
-    return pl.pallas_call(
-        lambda *refs: project_kernel(near, *refs),
-        grid=(blocks,),
-        in_specs=[
-            pl.BlockSpec((1, tokens, channels), lambda k: (k, 0, 0)),
-            pl.BlockSpec((1, tokens, channels), lambda k: (k, 0, 0)),
-            pl.BlockSpec((2 * channels, cols), lambda k: (k, 0)),
-        ],
-        out_specs=pl.BlockSpec((tokens, cols), lambda k: (0, 0)),
-        out_shape=jax.ShapeDtypeStruct((tokens, cols), BF16),
-        scratch_shapes=[pltpu.VMEM((tokens, cols), F32)],
+    parts = in_hbm(weight.reshape(blocks, near, 2, channels // near, cols))
+    in_specs = [
+        pl.BlockSpec((1, tokens, channels), lambda k, core: (k, 0, 0)),
+        pl.BlockSpec((1, near, 1, channels // near, cols), lambda k, core: (k, 0, core[0], 0, 0)),
+    ]
+    if before is None:
+        body = lambda c, f, w, o, acc: project_kernel(c, f, w, None, o, acc)
+        more = ()
+    else:
+        body = project_kernel
+        more = (before,)
+        in_specs.append(pl.BlockSpec((tokens, cols), lambda k, core: (0, 0)))
+    return pl.pallas_call(
+        body,
+        grid_spec=pltpu.PrefetchScalarGridSpec(
+            num_scalar_prefetch=1,
+            grid=(blocks,),
+            in_specs=in_specs,
+            out_specs=pl.BlockSpec((tokens, cols), lambda k, core: (0, 0)),
+            scratch_shapes=[pltpu.VMEM((tokens, cols), F32)],
+        ),
+        out_shape=jax.ShapeDtypeStruct((tokens, cols), F32 if before is None else BF16),
         name="project",
         compiler_params=pltpu.CompilerParams(vmem_limit_bytes=16 << 20),
-    )(own, other, weight)
+        cost_estimate=pl.CostEstimate(
+            flops=4_000_000_000, bytes_accessed=weight.size, transcendentals=0
+        ),
+    )(core, features, parts, *more)
 
 
 def next_tokens(value):
@@ -301,7 +308,7 @@
 
     copies = jnp.broadcast_to(out_weight[None], (lax.axis_size("zh"), *out_weight.shape))
     weight_rows = to_each(copies, "zh").reshape(-1, out_weight.shape[1])
-    weight = in_hbm(lax.all_gather(weight_rows, ("x", "y"), axis=0, tiled=True))
+    weight = lax.all_gather(weight_rows, ("x", "y"), axis=0, tiled=True)
     product = (value_in.astype(F32) * key_in.astype(F32)).astype(BF16)
     prior = next_tokens(product)
     bands = short_bands(short_filter)
@@ -313,7 +320,9 @@
     gated = gate_stage(returned, mid, gate_long, skip_gain[None, :], lax.axis_size("zl"), near)
     own = to_each(gated, "zl")
     other = lax.ppermute(own, "core", [(0, 1), (1, 0)])
-    return project(own, other, weight, near)
+    core = lax.axis_index("core").reshape(1)
+    half = project(own, weight, core, None, near)
+    return project(other, weight, 1 - core, half, near)
 
 
 def solution(mesh):

time: 150 us -> 151 us (level)
  Pallas kernels: 19 us -> 21.4 us
    pallas_call x1 -> x2, Pallas kernels: 4.21 us -> 6.59 us  [project(): pl.pallas_call(body, grid_spec=pltpu.PrefetchScalarGridSpec(num_scalar_pr...]
    ppermute x1, waiting for transfers between devices: 1.51 us -> 0.01 us  [shards(): other = lax.ppermute(own, 'core', [(0, 1), (1, 0)])]
  transfers between devices with their start and end apart: 4 -> 4, of which waited for: 3 -> 2; matrix products, arithmetic and copies ran while one was open for 1% -> 1% of each run, Pallas kernels for 10% -> 12%
where the time goes in v3:
time: 151 us; the launch traced here: 150 us
  blocking collectives  76.2 us (50%)
  starting transfers between devices  25.9 us (17%)
  Pallas kernels  21.4 us (14%)
  between operations  13.5 us (9%)
  waiting for transfers between devices  10.1 us (7%)
  local copies, waits for them, and re-layouts  1.56 us (1%)
    all_to_all x3, blocking collectives, to_each(): return lax.all_to_all(parts, axes, 0, 0, tiled=True)  76.2 us
    all_to_all x1, starting transfers between devices, to_each(): return lax.all_to_all(parts, axes, 0, 0, tiled=True)  16.5 us
    all_to_all x1, waiting for transfers between devices, to_each(): return lax.all_to_all(parts, axes, 0, 0, tiled=True)  9.16 us
    pallas_call x1, Pallas kernels, long_blocks(): pl.pallas_call(toeplitz_kernel, grid=(steps,), in_specs=[pl.BlockSpec((ro...  7.06 us
    pallas_call x2, Pallas kernels, project(): pl.pallas_call(body, grid_spec=pltpu.PrefetchScalarGridSpec(num_scalar_pr...  6.59 us
    ppermute x1, starting transfers between devices, shards(): other = lax.ppermute(own, 'core', [(0, 1), (1, 0)])  6.24 us
    pallas_call x1, Pallas kernels, long_stage(): pl.pallas_call(conv_kernel, grid=(rows // each,), in_specs=[pl.BlockSpec(...  5.16 us
    ppermute x1, starting transfers between devices, next_tokens(): return lax.ppermute(value, CTX, [(s, s + 1) for s in range(size - 1)])  3.21 us
  transfers between devices with their start and end apart: 4, of which 2 were waited for; matrix products, arithmetic and copies ran while one was open for 1% of the time, Pallas kernels for 12%

profile of v3, /device:TPU:1, one launch (start us, length us, event | category | flops | bytes accessed | tf_op | source)
XLA Modules:
  0.0 149.7 jit_solution(2859668956105658837)
XLA Ops:
  6.5 0.0 all-gather.2.cloned.1.call-start
  6.5 0.9 broadcast_in_dim.10
  7.4 0.0 copy-start
  7.4 29.9 %all_to_all.20 = bf16[4,64,512]{2,1,0:T(8,128)(2,1)} all-to-all(bf16[4,64,512]{2,1,0:T(8,128)(2,1)S(1)} %broadcast_in_dim.10), channel_id=1, replica_groups=mesh['x'=4,'zh'=4,'y'=4,'zl'=4,'core'=2] {'zh'}, dimensions={0} | all-to-all | bytes 524288 | tf_op jit(solution)/shard_map/all_to_all | solution.py:298
  37.3 0.0 all-gather.2.cloned.1.call-update
  37.3 1.0 multiply_convert_fusion.own_ref
  38.3 3.2 %collective-permute-start = (bf16[128,512]{1,0:T(8,128)(2,1)S(1)}, bf16[128,512]{1,0:T(8,128)(2,1)S(1)}, u32[]{:S(2)}, u32[]{:S(2)}) collective-permute-start(bf16[128,512]{1,0:T(8,128)(2,1)S(1)} %multiply_convert_fusion.own_ref), channel_id=1, source_target_pairs={{0,8},{8,16},{16,24},{24,32},{32,40},{40,48},{48,56},{56,64},{64,7... | collective-permute-start | bytes 393224 | tf_op jit(solution)/shard_map/ppermute | solution.py:290
  41.5 0.0 copy-start.2
  41.5 0.7 copy-done.2
  42.2 0.4 short_bands.1.band_ref
  42.6 0.9 collective-permute-done.prior_ref
  43.4 0.0 copy-done
  43.4 1.1 short_stage.1.refs_1_
  44.6 16.5 %all-to-all-start = ((bf16[64,8,128]{2,1,0:T(8,128)(2,1)}), bf16[64,8,128]{2,1,0:T(8,128)(2,1)S(1)}, u32[]{:S(2)}, u32[]{:S(2)}) async-start(bf16[64,8,128]{2,1,0:T(8,128)(2,1)} %bitcast.1), calls=%async_computation | async-start | bytes 262144 | tf_op jit(solution)/shard_map/all_to_all | solution.py:298
  61.0 7.1 %long_blocks.1.blk_ref = bf16[8,512,1024]{2,1,0:T(8,128)(2,1)} custom-call(f32[8,8192]{1,0:T(8,128)} %filt_ref.1), custom_call_target="tpu_custom_call" | custom-call | flops 4000000000 | bytes 8388608 | tf_op jit(solution)/shard_map/long_blocks/pallas_call | solution.py:103
  68.1 0.0 copy-start.1
  68.1 0.0 copy-start.3
  68.1 9.2 %all-to-all-done.sig_ref = bf16[64,8,128]{2,1,0:T(8,128)(2,1)S(1)} async-done(((bf16[64,8,128]{2,1,0:T(8,128)(2,1)}), bf16[64,8,128]{2,1,0:T(8,128)(2,1)S(1)}, u32[]{:S(2)}, u32[]{:S(2)}) %all-to-all-start) | async-done | bytes 131104 | tf_op jit(solution)/shard_map/all_to_all | solution.py:298
  77.3 5.2 %long_stage.1 = bf16[64,8,128]{2,1,0:T(8,128)(2,1)S(1)} custom-call(bf16[64,8,128]{2,1,0:T(8,128)(2,1)S(1)} %all-to-all-done.sig_ref, bf16[8,512,1024]{2,1,0:T(8,128)(2,1)} %long_blocks.1.blk_ref), custom_call_target="tpu_custom_call" | custom-call | flops 8000000000 | bytes 8388608 | tf_op jit(solution)/shard_map/long_stage/pallas_call | solution.py:179
  82.4 23.9 %all_to_all.21 = bf16[64,8,128]{2,1,0:T(8,128)(2,1)S(1)} all-to-all(bf16[64,8,128]{2,1,0:T(8,128)(2,1)S(1)} %long_stage.1), channel_id=1, replica_groups=mesh['x'=4,'zh'=4,'y'=4,'zl'=4,'core'=2] {'x','zh','y'}, dimensions={0} | all-to-all | bytes 262144 | tf_op jit(solution)/shard_map/all_to_all | solution.py:298
  106.3 0.0 copy-done.1
  106.3 0.0 copy-done.3
  106.3 1.2 gate_stage.1
  107.5 22.4 %all_to_all.22.f = bf16[4,128,512]{2,1,0:T(8,128)(2,1)S(1)} all-to-all(bf16[4,128,512]{2,1,0:T(8,128)(2,1)S(1)} %gate_stage.1), channel_id=1, replica_groups=mesh['x'=4,'zh'=4,'y'=4,'zl'=4,'core'=2] {'zl'}, dimensions={0} | all-to-all | bytes 1048576 | tf_op jit(solution)/shard_map/all_to_all | solution.py:298
  129.9 6.2 %collective-permute-start.1 = (bf16[4,128,512]{2,1,0:T(8,128)(2,1)S(1)}, bf16[4,128,512]{2,1,0:T(8,128)(2,1)S(1)}, u32[]{:S(2)}, u32[]{:S(2)}) collective-permute-start(bf16[4,128,512]{2,1,0:T(8,128)(2,1)S(1)} %all_to_all.22.f), channel_id=1, source_target_pairs={{0,1},{1,0},{2,3},{3,2},{4,5},{5,4},{6,7},{7,6},{8,9},{9,8},{10,11... | collective-permute-start | bytes 1572872 | tf_op jit(solution)/shard_map/ppermute | solution.py:322
  136.2 0.0 all-gather.2.cloned.1.call-done
  136.2 3.0 %project.2.refs_2_ = f32[128,512]{1,0:T(8,128)S(1)} custom-call(s32[1]{0:T(128)} %bitcast.c, bf16[4,128,512]{2,1,0:T(8,128)(2,1)S(1)} %all_to_all.22.f, bf16[4,4,2,128,512]{4,3,2,1,0:T(8,128)(2,1)} %bitcast.9), custom_call_target="tpu_custom_call" | custom-call | flops 4000000000 | bytes 2097152 | tf_op jit(solution)/shard_map/project/pallas_call | solution.py:270
  139.2 0.0 collective-permute-done.1.refs_0_
  139.2 3.6 %project.3 = bf16[128,512]{1,0:T(8,128)(2,1)} custom-call(s32[1]{0:T(128)S(6)} %sub.3.core_ref, bf16[4,128,512]{2,1,0:T(8,128)(2,1)S(1)} %collective-permute-done.1.refs_0_, bf16[4,4,2,128,512]{4,3,2,1,0:T(8,128)(2,1)} %bitcast.10, f32[128,512]{1,0:T(8,128)S(1)} %project.2.refs_2_), custom_call_target="tpu_custom_call" | custom-call | flops 4000000000 | bytes 2097152 | tf_op jit(solution)/shard_map/project/pallas_call | solution.py:270
Async XLA Ops:
  6.5 129.7 %all-gather.2.cloned.1.call-start = ((), (), s32[]{:S(2)}) async-start(), calls=%async_computation.4 | async-start | bytes 4456448 | tf_op jit(solution)/shard_map/all_gather | solution.py:311
  7.4 36.1 %copy-start = (bf16[128,512]{1,0:T(8,128)(2,1)S(1)}, bf16[128,512]{1,0:T(8,128)(2,1)}, u32[]{:S(2)}) copy-start(bf16[128,512]{1,0:T(8,128)(2,1)} %gate_ref.1) | copy-start | bytes 393220
  38.3 5.1 %collective-permute-start = (bf16[128,512]{1,0:T(8,128)(2,1)S(1)}, bf16[128,512]{1,0:T(8,128)(2,1)S(1)}, u32[]{:S(2)}, u32[]{:S(2)}) collective-permute-start(bf16[128,512]{1,0:T(8,128)(2,1)S(1)} %multiply_convert_fusion.own_ref), channel_id=1, source_target_pairs={{0,8},{8,16},{16,24},{24,32},{32,40},{40,48},{48,56},{56,64},{64,7... | collective-permute-start | bytes 393224 | tf_op jit(solution)/shard_map/ppermute | solution.py:290
  41.5 0.7 copy-start.2
  44.6 32.7 %all-to-all-start = ((bf16[64,8,128]{2,1,0:T(8,128)(2,1)}), bf16[64,8,128]{2,1,0:T(8,128)(2,1)S(1)}, u32[]{:S(2)}, u32[]{:S(2)}) async-start(bf16[64,8,128]{2,1,0:T(8,128)(2,1)} %bitcast.1), calls=%async_computation | async-start | bytes 262144 | tf_op jit(solution)/shard_map/all_to_all | solution.py:298
  68.1 38.2 %copy-start.1 = (bf16[128,512]{1,0:T(8,128)(2,1)S(1)}, bf16[128,512]{1,0:T(8,128)(2,1)}, u32[]{:S(2)}) copy-start(bf16[128,512]{1,0:T(8,128)(2,1)} %refs_2_.1) | copy-start | bytes 393220
  68.1 38.2 %copy-start.3 = (f32[512]{0:T(512)S(1)}, f32[512]{0:T(512)}, u32[]{:S(2)}) copy-start(f32[512]{0:T(512)} %param.14) | copy-start | bytes 6148
  129.9 9.3 %collective-permute-start.1 = (bf16[4,128,512]{2,1,0:T(8,128)(2,1)S(1)}, bf16[4,128,512]{2,1,0:T(8,128)(2,1)S(1)}, u32[]{:S(2)}, u32[]{:S(2)}) collective-permute-start(bf16[4,128,512]{2,1,0:T(8,128)(2,1)S(1)} %all_to_all.22.f), channel_id=1, source_target_pairs={{0,1},{1,0},{2,3},{3,2},{4,5},{5,4},{6,7},{7,6},{8,9},{9,8},{10,11... | collective-permute-start | bytes 1572872 | tf_op jit(solution)/shard_map/ppermute | solution.py:322
Sparse Core Ops, SparseCore 0:
  37.4 67.3 all-gather.1

commit v4 on v3

--- a/solution.py
+++ b/solution.py
@@ -79,7 +79,7 @@
     )(prior, own, gate, band)
 
 
-def toeplitz_kernel(filt_ref, out_ref, last):
+def toeplitz_kernel(filt_ref, after_ref, out_ref, last):
     own = upper(HALF)
 
     @pl.when(pl.program_id(0) == 0)
@@ -96,14 +96,17 @@
         last[c] = before
 
 
-def long_blocks(long_filter):
+def long_blocks(long_filter, after):
     rows, seq = long_filter.shape
     steps = 8
     wide = seq // steps
     return pl.pallas_call(
         toeplitz_kernel,
         grid=(steps,),
-        in_specs=[pl.BlockSpec((rows, wide), lambda j: (0, j))],
+        in_specs=[
+            pl.BlockSpec((rows, wide), lambda j: (0, j)),
+            pl.BlockSpec(memory_space=pl.ANY),
+        ],
         out_specs=pl.BlockSpec((rows, HALF, wide), lambda j: (0, j, 0)),
         out_shape=jax.ShapeDtypeStruct((rows, steps * HALF, wide), BF16),
         scratch_shapes=[pltpu.VMEM((rows, HALF, LANES), F32)],
@@ -112,7 +115,7 @@
         cost_estimate=pl.CostEstimate(
             flops=4_000_000_000, bytes_accessed=rows * steps * HALF * wide * 2, transcendentals=0
         ),
-    )(long_filter)
+    )(long_filter, after)
 
 
 def moved_down(x, rows):
@@ -285,6 +288,48 @@
     )(core, features, parts, *more)
 
 
+def placed_kernel(*refs):
+    *value_refs, out_ref, mark_ref, sems = refs
+    me = lax.axis_index("zh")
+    size = len(value_refs)
+    copies = [
+        pltpu.make_async_copy(ref, out_ref.at[lax.rem(me + size - k, size)], sems.at[k])
+        for k, ref in enumerate(value_refs)
+    ]
+    for copy in copies:
+        copy.start()
+    mark_ref[...] = jnp.zeros(mark_ref.shape, F32)
+    for copy in copies:
+        copy.wait()
+
+
+def placed(values):
+    shape = values[0].shape
+    return pl.pallas_call(
+        placed_kernel,
+        out_shape=(
+            jax.ShapeDtypeStruct((len(values), *shape), values[0].dtype),
+            jax.ShapeDtypeStruct((8, LANES), F32),
+        ),
+        in_specs=[pl.BlockSpec(memory_space=pltpu.VMEM)] * len(values),
+        out_specs=(
+            pl.BlockSpec(memory_space=pltpu.HBM),
+            pl.BlockSpec(memory_space=pltpu.VMEM),
+        ),
+        scratch_shapes=[pltpu.SemaphoreType.DMA((len(values),))],
+        name="placed",
+        compiler_params=pltpu.CompilerParams(vmem_limit_bytes=4 << 20),
+        cost_estimate=pl.CostEstimate(
+            flops=100_000_000, bytes_accessed=values[0].size * 16, transcendentals=0
+        ),
+    )(*values)
+
+
+def passed_round(value, axis, steps):
+    size = lax.axis_size(axis)
+    return lax.ppermute(value, axis, [(s, (s + steps) % size) for s in range(size)])
+
+
 def next_tokens(value):
     size = lax.axis_size(CTX)
     return lax.ppermute(value, CTX, [(s, s + 1) for s in range(size - 1)])
@@ -306,15 +351,18 @@
     per_dev = channels // ways
     near = lax.axis_size("y")
 
-    copies = jnp.broadcast_to(out_weight[None], (lax.axis_size("zh"), *out_weight.shape))
-    weight_rows = to_each(copies, "zh").reshape(-1, out_weight.shape[1])
+    far2 = passed_round(out_weight, "zh", 2)
+    far1 = passed_round(out_weight, "zh", 1)
+    far3 = passed_round(out_weight, "zh", 3)
+    weight_rows, mark = placed([out_weight, far1, far2, far3])
+    weight_rows = weight_rows.reshape(-1, out_weight.shape[1])
     weight = lax.all_gather(weight_rows, ("x", "y"), axis=0, tiled=True)
     product = (value_in.astype(F32) * key_in.astype(F32)).astype(BF16)
     prior = next_tokens(product)
     bands = short_bands(short_filter)
     mid = short_stage(prior, product, gate_short, bands)
     spread = to_each(mid.reshape(ways, per_dev, tokens), CTX)
-    blocks = in_hbm(long_blocks(long_filter))
+    blocks = in_hbm(long_blocks(long_filter, mark))
     long_part = long_stage(spread, blocks)
     returned = to_each(long_part, CTX).reshape(channels, tokens)
     gated = gate_stage(returned, mid, gate_long, skip_gain[None, :], lax.axis_size("zl"), near)

time: 151 us -> 158 us (1.046)
  blocking collectives: 76.2 us -> 38.6 us
  starting transfers between devices: 25.9 us -> 59 us
  waiting for transfers between devices: 10.1 us -> 20.3 us
    all_to_all x3 -> x2, blocking collectives: 76.2 us -> 38.6 us  [to_each(): return lax.all_to_all(parts, axes, 0, 0, tiled=True)]
    ppermute x0 -> x3, starting transfers between devices: none -> 25.6 us  [passed_round(): lax.ppermute(value, axis, [(s, (s + steps) % size) for s in range(size)])]
    ppermute x0 -> x3, waiting for transfers between devices: none -> 9.07 us  [passed_round(): lax.ppermute(value, axis, [(s, (s + steps) % size) for s in range(size)])]
    all_to_all x1, starting transfers between devices: 16.5 us -> 25.3 us  [to_each(): return lax.all_to_all(parts, axes, 0, 0, tiled=True)]
  transfers between devices with their start and end apart: 4 -> 7, of which waited for: 2 -> 4; matrix products, arithmetic and copies ran while one was open for 1% -> 1% of each run, Pallas kernels for 12% -> 11%
where the time goes in v4:
time: 158 us; the launch traced here: 157 us
  starting transfers between devices  59 us (37%)
  blocking collectives  38.6 us (24%)
  Pallas kernels  22.2 us (14%)
  waiting for transfers between devices  20.3 us (13%)
  between operations  13.5 us (9%)
  local copies, waits for them, and re-layouts  2.13 us (1%)
    all_to_all x2, blocking collectives, to_each(): return lax.all_to_all(parts, axes, 0, 0, tiled=True)  38.6 us
    ppermute x3, starting transfers between devices, passed_round(): lax.ppermute(value, axis, [(s, (s + steps) % size) for s in range(size)])  25.6 us
    all_to_all x1, starting transfers between devices, to_each(): return lax.all_to_all(parts, axes, 0, 0, tiled=True)  25.3 us
    all_to_all x1, waiting for transfers between devices, to_each(): return lax.all_to_all(parts, axes, 0, 0, tiled=True)  9.94 us
    ppermute x3, waiting for transfers between devices, passed_round(): lax.ppermute(value, axis, [(s, (s + steps) % size) for s in range(size)])  9.07 us
    pallas_call x1, Pallas kernels, long_blocks(): pl.pallas_call(toeplitz_kernel, grid=(steps,), in_specs=[pl.BlockSpec((ro...  6.96 us
    pallas_call x2, Pallas kernels, project(): pl.pallas_call(body, grid_spec=pltpu.PrefetchScalarGridSpec(num_scalar_pr...  6.59 us
    pallas_call x1, Pallas kernels, long_stage(): pl.pallas_call(conv_kernel, grid=(rows // each,), in_specs=[pl.BlockSpec(...  5.28 us
  transfers between devices with their start and end apart: 7, of which 4 were waited for; matrix products, arithmetic and copies ran while one was open for 1% of the time, Pallas kernels for 11%

profile of v4, /device:TPU:1, one launch (start us, length us, event | category | flops | bytes accessed | tf_op | source)
XLA Modules:
  0.0 156.7 jit_solution(18117124183079583819)
XLA Ops:
  6.5 0.0 copy-start
  6.5 0.0 all-gather.2.cloned.1.call-start
  6.5 9.8 %collective-permute-start.1 = (bf16[64,512]{1,0:T(8,128)(2,1)}, bf16[64,512]{1,0:T(8,128)(2,1)S(1)}, u32[]{:S(2)}, u32[]{:S(2)}) collective-permute-start(bf16[64,512]{1,0:T(8,128)(2,1)} %refs_0_.1), channel_id=1, source_target_pairs={{0,32},{32,64},{64,96},{96,0},{1,33},{33,65},{65,97},{97,1},{2,34}... | collective-permute-start | bytes 196616 | tf_op jit(solution)/shard_map/ppermute | solution.py:330
  16.3 10.6 %collective-permute-start.2 = (bf16[64,512]{1,0:T(8,128)(2,1)}, bf16[64,512]{1,0:T(8,128)(2,1)S(1)}, u32[]{:S(2)}, u32[]{:S(2)}) collective-permute-start(bf16[64,512]{1,0:T(8,128)(2,1)} %refs_0_.1), channel_id=1, source_target_pairs={{0,64},{32,96},{64,0},{96,32},{1,65},{33,97},{65,1},{97,33},{2,66}... | collective-permute-start | bytes 196616 | tf_op jit(solution)/shard_map/ppermute | solution.py:330
  26.9 5.2 %collective-permute-start.3 = (bf16[64,512]{1,0:T(8,128)(2,1)}, bf16[64,512]{1,0:T(8,128)(2,1)S(1)}, u32[]{:S(2)}, u32[]{:S(2)}) collective-permute-start(bf16[64,512]{1,0:T(8,128)(2,1)} %refs_0_.1), channel_id=1, source_target_pairs={{0,96},{32,0},{64,32},{96,64},{1,97},{33,1},{65,33},{97,65},{2,98}... | collective-permute-start | bytes 196616 | tf_op jit(solution)/shard_map/ppermute | solution.py:330
  32.1 0.0 collective-permute-done.1.refs_1_
  32.1 2.2 %collective-permute-done.2.refs_2_ = bf16[64,512]{1,0:T(8,128)(2,1)S(1)} collective-permute-done((bf16[64,512]{1,0:T(8,128)(2,1)}, bf16[64,512]{1,0:T(8,128)(2,1)S(1)}, u32[]{:S(2)}, u32[]{:S(2)}) %collective-permute-start.2) | collective-permute-done | bytes 65568 | tf_op jit(solution)/shard_map/ppermute | solution.py:330
  34.3 6.9 %collective-permute-done.3.refs_3_ = bf16[64,512]{1,0:T(8,128)(2,1)S(1)} collective-permute-done((bf16[64,512]{1,0:T(8,128)(2,1)}, bf16[64,512]{1,0:T(8,128)(2,1)S(1)}, u32[]{:S(2)}, u32[]{:S(2)}) %collective-permute-start.3) | collective-permute-done | bytes 65568 | tf_op jit(solution)/shard_map/ppermute | solution.py:330
  41.2 0.0 copy-start.2
  41.2 0.8 copy-done.2
  42.0 0.8 placed.1
  42.8 0.0 copy-start.5
  42.8 0.6 copy-done.5
  43.4 0.0 all-gather.2.cloned.1.call-update
  43.4 1.0 multiply_convert_fusion.own_ref
  44.4 3.2 %collective-permute-start = (bf16[128,512]{1,0:T(8,128)(2,1)S(1)}, bf16[128,512]{1,0:T(8,128)(2,1)S(1)}, u32[]{:S(2)}, u32[]{:S(2)}) collective-permute-start(bf16[128,512]{1,0:T(8,128)(2,1)S(1)} %multiply_convert_fusion.own_ref), channel_id=1, source_target_pairs={{0,8},{8,16},{16,24},{24,32},{32,40},{40,48},{48,56},{56,64},{64,7... | collective-permute-start | bytes 393224 | tf_op jit(solution)/shard_map/ppermute | solution.py:335
  47.7 0.0 copy-start.3
  47.7 0.7 copy-done.3
  48.4 0.4 short_bands.1.band_ref
  48.7 1.3 collective-permute-done.prior_ref
  50.0 0.0 copy-done
  50.0 1.1 short_stage.1.refs_1_
  51.1 25.3 %all-to-all-start = ((bf16[64,8,128]{2,1,0:T(8,128)(2,1)}), bf16[64,8,128]{2,1,0:T(8,128)(2,1)S(1)}, u32[]{:S(2)}, u32[]{:S(2)}) async-start(bf16[64,8,128]{2,1,0:T(8,128)(2,1)} %bitcast.1), calls=%async_computation | async-start | bytes 262144 | tf_op jit(solution)/shard_map/all_to_all | solution.py:343
  76.4 7.0 %long_blocks.1.blk_ref = bf16[8,512,1024]{2,1,0:T(8,128)(2,1)} custom-call(f32[8,8192]{1,0:T(8,128)} %filt_ref.1, f32[8,128]{1,0:T(8,128)} %copy-done.5), custom_call_target="tpu_custom_call" | custom-call | flops 4000000000 | bytes 8388608 | tf_op jit(solution)/shard_map/long_blocks/pallas_call | solution.py:103
  83.4 0.0 copy-start.1
  83.4 0.0 copy-start.4
  83.4 9.9 %all-to-all-done.sig_ref = bf16[64,8,128]{2,1,0:T(8,128)(2,1)S(1)} async-done(((bf16[64,8,128]{2,1,0:T(8,128)(2,1)}), bf16[64,8,128]{2,1,0:T(8,128)(2,1)S(1)}, u32[]{:S(2)}, u32[]{:S(2)}) %all-to-all-start) | async-done | bytes 131104 | tf_op jit(solution)/shard_map/all_to_all | solution.py:343
  93.3 5.3 %long_stage.1 = bf16[64,8,128]{2,1,0:T(8,128)(2,1)S(1)} custom-call(bf16[64,8,128]{2,1,0:T(8,128)(2,1)S(1)} %all-to-all-done.sig_ref, bf16[8,512,1024]{2,1,0:T(8,128)(2,1)} %long_blocks.1.blk_ref), custom_call_target="tpu_custom_call" | custom-call | flops 8000000000 | bytes 8388608 | tf_op jit(solution)/shard_map/long_stage/pallas_call | solution.py:182
  98.6 23.7 %all_to_all.15 = bf16[64,8,128]{2,1,0:T(8,128)(2,1)S(1)} all-to-all(bf16[64,8,128]{2,1,0:T(8,128)(2,1)S(1)} %long_stage.1), channel_id=1, replica_groups=mesh['x'=4,'zh'=4,'y'=4,'zl'=4,'core'=2] {'x','zh','y'}, dimensions={0} | all-to-all | bytes 262144 | tf_op jit(solution)/shard_map/all_to_all | solution.py:343
  122.3 0.0 copy-done.1
  122.3 0.0 copy-done.4
  122.3 1.2 gate_stage.1
  123.5 14.8 %all_to_all.16.f = bf16[4,128,512]{2,1,0:T(8,128)(2,1)S(1)} all-to-all(bf16[4,128,512]{2,1,0:T(8,128)(2,1)S(1)} %gate_stage.1), channel_id=1, replica_groups=mesh['x'=4,'zh'=4,'y'=4,'zl'=4,'core'=2] {'zl'}, dimensions={0} | all-to-all | bytes 1048576 | tf_op jit(solution)/shard_map/all_to_all | solution.py:343
  138.3 4.9 %collective-permute-start.4 = (bf16[4,128,512]{2,1,0:T(8,128)(2,1)S(1)}, bf16[4,128,512]{2,1,0:T(8,128)(2,1)S(1)}, u32[]{:S(2)}, u32[]{:S(2)}) collective-permute-start(bf16[4,128,512]{2,1,0:T(8,128)(2,1)S(1)} %all_to_all.16.f), channel_id=1, source_target_pairs={{0,1},{1,0},{2,3},{3,2},{4,5},{5,4},{6,7},{7,6},{8,9},{9,8},{10,11... | collective-permute-start | bytes 1572872 | tf_op jit(solution)/shard_map/ppermute | solution.py:370
  143.2 0.0 all-gather.2.cloned.1.call-done
  143.3 3.0 %project.2.refs_2_ = f32[128,512]{1,0:T(8,128)S(1)} custom-call(s32[1]{0:T(128)} %bitcast.c, bf16[4,128,512]{2,1,0:T(8,128)(2,1)S(1)} %all_to_all.16.f, bf16[4,4,2,128,512]{4,3,2,1,0:T(8,128)(2,1)} %bitcast.8), custom_call_target="tpu_custom_call" | custom-call | flops 4000000000 | bytes 2097152 | tf_op jit(solution)/shard_map/project/pallas_call | solution.py:273
  146.2 0.0 collective-permute-done.4.refs_0_
  146.2 3.6 %project.3 = bf16[128,512]{1,0:T(8,128)(2,1)} custom-call(s32[1]{0:T(128)S(6)} %sub.3.core_ref, bf16[4,128,512]{2,1,0:T(8,128)(2,1)S(1)} %collective-permute-done.4.refs_0_, bf16[4,4,2,128,512]{4,3,2,1,0:T(8,128)(2,1)} %bitcast.9, f32[128,512]{1,0:T(8,128)S(1)} %project.2.refs_2_), custom_call_target="tpu_custom_call" | custom-call | flops 4000000000 | bytes 2097152 | tf_op jit(solution)/shard_map/project/pallas_call | solution.py:273
Async XLA Ops:
  6.5 43.4 %copy-start = (bf16[128,512]{1,0:T(8,128)(2,1)S(1)}, bf16[128,512]{1,0:T(8,128)(2,1)}, u32[]{:S(2)}) copy-start(bf16[128,512]{1,0:T(8,128)(2,1)} %gate_ref.1) | copy-start | bytes 393220
  6.5 136.7 %all-gather.2.cloned.1.call-start = ((), (), s32[]{:S(2)}) async-start(), calls=%async_computation.3 | async-start | bytes 4456448 | tf_op jit(solution)/shard_map/all_gather | solution.py:359
  6.5 25.6 %collective-permute-start.1 = (bf16[64,512]{1,0:T(8,128)(2,1)}, bf16[64,512]{1,0:T(8,128)(2,1)S(1)}, u32[]{:S(2)}, u32[]{:S(2)}) collective-permute-start(bf16[64,512]{1,0:T(8,128)(2,1)} %refs_0_.1), channel_id=1, source_target_pairs={{0,32},{32,64},{64,96},{96,0},{1,33},{33,65},{65,97},{97,1},{2,34}... | collective-permute-start | bytes 196616 | tf_op jit(solution)/shard_map/ppermute | solution.py:330
  16.3 18.0 %collective-permute-start.2 = (bf16[64,512]{1,0:T(8,128)(2,1)}, bf16[64,512]{1,0:T(8,128)(2,1)S(1)}, u32[]{:S(2)}, u32[]{:S(2)}) collective-permute-start(bf16[64,512]{1,0:T(8,128)(2,1)} %refs_0_.1), channel_id=1, source_target_pairs={{0,64},{32,96},{64,0},{96,32},{1,65},{33,97},{65,1},{97,33},{2,66}... | collective-permute-start | bytes 196616 | tf_op jit(solution)/shard_map/ppermute | solution.py:330
  26.9 14.3 %collective-permute-start.3 = (bf16[64,512]{1,0:T(8,128)(2,1)}, bf16[64,512]{1,0:T(8,128)(2,1)S(1)}, u32[]{:S(2)}, u32[]{:S(2)}) collective-permute-start(bf16[64,512]{1,0:T(8,128)(2,1)} %refs_0_.1), channel_id=1, source_target_pairs={{0,96},{32,0},{64,32},{96,64},{1,97},{33,1},{65,33},{97,65},{2,98}... | collective-permute-start | bytes 196616 | tf_op jit(solution)/shard_map/ppermute | solution.py:330
  41.2 0.8 copy-start.2
  42.8 0.6 copy-start.5
  44.4 5.5 %collective-permute-start = (bf16[128,512]{1,0:T(8,128)(2,1)S(1)}, bf16[128,512]{1,0:T(8,128)(2,1)S(1)}, u32[]{:S(2)}, u32[]{:S(2)}) collective-permute-start(bf16[128,512]{1,0:T(8,128)(2,1)S(1)} %multiply_convert_fusion.own_ref), channel_id=1, source_target_pairs={{0,8},{8,16},{16,24},{24,32},{32,40},{40,48},{48,56},{56,64},{64,7... | collective-permute-start | bytes 393224 | tf_op jit(solution)/shard_map/ppermute | solution.py:335
  47.7 0.7 copy-start.3
  51.1 42.2 %all-to-all-start = ((bf16[64,8,128]{2,1,0:T(8,128)(2,1)}), bf16[64,8,128]{2,1,0:T(8,128)(2,1)S(1)}, u32[]{:S(2)}, u32[]{:S(2)}) async-start(bf16[64,8,128]{2,1,0:T(8,128)(2,1)} %bitcast.1), calls=%async_computation | async-start | bytes 262144 | tf_op jit(solution)/shard_map/all_to_all | solution.py:343
  83.4 38.9 %copy-start.1 = (bf16[128,512]{1,0:T(8,128)(2,1)S(1)}, bf16[128,512]{1,0:T(8,128)(2,1)}, u32[]{:S(2)}) copy-start(bf16[128,512]{1,0:T(8,128)(2,1)} %refs_2_.1) | copy-start | bytes 393220
  83.4 38.9 %copy-start.4 = (f32[512]{0:T(512)S(1)}, f32[512]{0:T(512)}, u32[]{:S(2)}) copy-start(f32[512]{0:T(512)} %param.14) | copy-start | bytes 6148
  138.3 7.9 %collective-permute-start.4 = (bf16[4,128,512]{2,1,0:T(8,128)(2,1)S(1)}, bf16[4,128,512]{2,1,0:T(8,128)(2,1)S(1)}, u32[]{:S(2)}, u32[]{:S(2)}) collective-permute-start(bf16[4,128,512]{2,1,0:T(8,128)(2,1)S(1)} %all_to_all.16.f), channel_id=1, source_target_pairs={{0,1},{1,0},{2,3},{3,2},{4,5},{5,4},{6,7},{7,6},{8,9},{9,8},{10,11... | collective-permute-start | bytes 1572872 | tf_op jit(solution)/shard_map/ppermute | solution.py:370
Sparse Core Ops, SparseCore 0:
  43.6 64.8 all-gather.1

commit v5 on v3

--- a/solution.py
+++ b/solution.py
@@ -23,6 +23,50 @@
     at = lax.broadcasted_iota(jnp.int32, (rows, LANES), 0)
     cols = lax.broadcasted_iota(jnp.int32, (rows, LANES), 1)
     return cols >= at
+
+
+def front_kernel(value_hbm, key_hbm, weight_hbm, product_ref, copies_ref, value, key, weight, sems):
+    loads = [
+        pltpu.make_async_copy(source, target, sems.at[0, k])
+        for k, (source, target) in enumerate(
+            ((weight_hbm, weight), (value_hbm, value), (key_hbm, key))
+        )
+    ]
+    for load in loads:
+        load.start()
+    loads[0].wait()
+    sends = [
+        pltpu.make_async_copy(weight, copies_ref.at[k], sems.at[1, k])
+        for k in range(copies_ref.shape[0])
+    ]
+    for send in sends:
+        send.start()
+    loads[1].wait()
+    loads[2].wait()
+    product_ref[...] = (value[...].astype(F32) * key[...].astype(F32)).astype(BF16)
+    for send in sends:
+        send.wait()
+
+
+def front(value, key, weight, count):
+    hbm = pl.BlockSpec(memory_space=pltpu.HBM)
+    return pl.pallas_call(
+        front_kernel,
+        in_specs=[hbm] * 3,
+        out_specs=(pl.BlockSpec(memory_space=pltpu.VMEM), hbm),
+        out_shape=(
+            jax.ShapeDtypeStruct(value.shape, BF16),
+            jax.ShapeDtypeStruct((count, *weight.shape), weight.dtype),
+        ),
+        scratch_shapes=[
+            pltpu.VMEM(value.shape, BF16),
+            pltpu.VMEM(key.shape, BF16),
+            pltpu.VMEM(weight.shape, weight.dtype),
+            pltpu.SemaphoreType.DMA((2, max(count, 3))),
+        ],
+        name="front",
+        compiler_params=pltpu.CompilerParams(vmem_limit_bytes=4 << 20),
+    )(in_hbm(value), in_hbm(key), in_hbm(weight))
 
 
 def band_kernel(taps_ref, band_ref):
@@ -154,47 +198,40 @@
     return even + jnp.where(low, turned_down(odd, 1, at), odd)
 
 
-def conv_kernel(sig_ref, blk_ref, out_ref, sig, acc):
-    step = pl.program_id(0)
+def conv_kernel(sig_ref, blk_hbm, out_ref, sig, acc, blk, sems):
     count, rows = sig_ref.shape[0], sig_ref.shape[1]
-    each = blk_ref.shape[0]
-
-    @pl.when(step == 0)
-    def _():
-        sig[...] = sig_ref[...].reshape(count * rows, LANES).astype(F32)
-
-    for i in range(each):
-        at = pl.ds(step * each + i, count, stride=rows)
-        acc[at, :] = conv_channel(sig[at, :], blk_ref, i)
-
-    @pl.when(step == pl.num_programs(0) - 1)
-    def _():
-        out_ref[...] = acc[...].reshape(count, rows, LANES).astype(BF16)
+    loads = [pltpu.make_async_copy(blk_hbm.at[c], blk.at[c], sems.at[c]) for c in range(rows)]
+    for load in loads:
+        load.start()
+    sig[...] = sig_ref[...].reshape(count * rows, LANES).astype(F32)
+    for c in range(rows):
+        at = pl.ds(c, count, stride=rows)
+        u = sig[at, :]
+        loads[c].wait()
+        acc[at, :] = conv_channel(u, blk, c)
+    out_ref[...] = acc[...].reshape(count, rows, LANES).astype(BF16)
 
 
 def long_stage(signal, blocks):
     count, rows, _ = signal.shape
-    _, deep, wide = blocks.shape
-    each = 2
+    vmem = pl.BlockSpec(memory_space=pltpu.VMEM)
     return pl.pallas_call(
         conv_kernel,
-        grid=(rows // each,),
-        in_specs=[
-            pl.BlockSpec((count, rows, LANES), lambda c: (0, 0, 0)),
-            pl.BlockSpec((each, deep, wide), lambda c: (c, 0, 0)),
-        ],
-        out_specs=pl.BlockSpec((count, rows, LANES), lambda c: (0, 0, 0)),
+        in_specs=[vmem, pl.BlockSpec(memory_space=pltpu.HBM)],
+        out_specs=vmem,
         out_shape=jax.ShapeDtypeStruct(signal.shape, BF16),
         scratch_shapes=[
             pltpu.VMEM((count * rows, LANES), F32),
             pltpu.VMEM((count * rows, LANES), F32),
+            pltpu.VMEM(blocks.shape, BF16),
+            pltpu.SemaphoreType.DMA((rows,)),
         ],
         name="long_stage",
-        compiler_params=pltpu.CompilerParams(vmem_limit_bytes=16 << 20),
-        cost_estimate=pl.CostEstimate(
-            flops=8_000_000_000, bytes_accessed=rows * deep * wide * 2, transcendentals=0
-        ),
-    )(signal, blocks)
+        compiler_params=pltpu.CompilerParams(vmem_limit_bytes=24 << 20),
+        cost_estimate=pl.CostEstimate(
+            flops=8_000_000_000, bytes_accessed=blocks.size * 2, transcendentals=0
+        ),
+    )(signal, in_hbm(blocks))
 
 
 def gate_kernel(near, long_ref, mid_ref, gate_ref, skip_ref, out_ref):
@@ -232,57 +269,73 @@
     )(long_rows, mid_rows, gate, skip)
 
 
-def project_kernel(core_ref, *refs):
-    feature_ref, weight_ref, before_ref, out_ref, acc = refs
-    k = pl.program_id(0)
-    rows = weight_ref.shape[1] * weight_ref.shape[3]
-    weight = weight_ref[...].reshape(rows, weight_ref.shape[4])
-    part = jnp.dot(feature_ref[0], weight, preferred_element_type=F32)
-
-    @pl.when(k == 0)
-    def _():
-        acc[...] = part if before_ref is None else before_ref[...] + part
-
-    @pl.when(k > 0)
-    def _():
-        acc[...] += part
-
-    @pl.when(k == pl.num_programs(0) - 1)
-    def _():
-        out_ref[...] = acc[...].astype(out_ref.dtype)
-
-
-def project(features, weight, core, before, near):
+def project_own_kernel(feature_ref, weight_ref, part_ref, rest_ref, held, sems):
+    core = lax.axis_index("core")
+    blocks = feature_ref.shape[0]
+    mine = [
+        pltpu.make_async_copy(weight_ref.at[k, :, core], held.at[k], sems.at[0, k])
+        for k in range(blocks)
+    ]
+    rest = [
+        pltpu.make_async_copy(weight_ref.at[k, :, 1 - core], rest_ref.at[k], sems.at[1, k])
+        for k in range(blocks)
+    ]
+    for copy in mine + rest:
+        copy.start()
+    total = jnp.zeros(part_ref.shape, F32)
+    for k in range(blocks):
+        mine[k].wait()
+        weight = held[k].reshape(feature_ref.shape[2], part_ref.shape[1])
+        total += jnp.dot(feature_ref[k], weight, preferred_element_type=F32)
+    part_ref[...] = total
+    for copy in rest:
+        copy.wait()
+
+
+def project_own(features, weight, near):
     blocks, tokens, channels = features.shape
     cols = weight.shape[1]
     parts = in_hbm(weight.reshape(blocks, near, 2, channels // near, cols))
-    in_specs = [
-        pl.BlockSpec((1, tokens, channels), lambda k, core: (k, 0, 0)),
-        pl.BlockSpec((1, near, 1, channels // near, cols), lambda k, core: (k, 0, core[0], 0, 0)),
-    ]
-    if before is None:
-        body = lambda c, f, w, o, acc: project_kernel(c, f, w, None, o, acc)
-        more = ()
-    else:
-        body = project_kernel
-        more = (before,)
-        in_specs.append(pl.BlockSpec((tokens, cols), lambda k, core: (0, 0)))
-    return pl.pallas_call(
-        body,
-        grid_spec=pltpu.PrefetchScalarGridSpec(
-            num_scalar_prefetch=1,
-            grid=(blocks,),
-            in_specs=in_specs,
-            out_specs=pl.BlockSpec((tokens, cols), lambda k, core: (0, 0)),
-            scratch_shapes=[pltpu.VMEM((tokens, cols), F32)],
-        ),
-        out_shape=jax.ShapeDtypeStruct((tokens, cols), F32 if before is None else BF16),
-        name="project",
-        compiler_params=pltpu.CompilerParams(vmem_limit_bytes=16 << 20),
-        cost_estimate=pl.CostEstimate(
-            flops=4_000_000_000, bytes_accessed=weight.size, transcendentals=0
-        ),
-    )(core, features, parts, *more)
+    vmem = pl.BlockSpec(memory_space=pltpu.VMEM)
+    half = (blocks, near, channels // near, cols)
+    return pl.pallas_call(
+        project_own_kernel,
+        in_specs=[vmem, pl.BlockSpec(memory_space=pltpu.HBM)],
+        out_specs=(vmem, vmem),
+        out_shape=(
+            jax.ShapeDtypeStruct((tokens, cols), F32),
+            jax.ShapeDtypeStruct(half, weight.dtype),
+        ),
+        scratch_shapes=[
+            pltpu.VMEM(half, weight.dtype),
+            pltpu.SemaphoreType.DMA((2, blocks)),
+        ],
+        name="project_own",
+        compiler_params=pltpu.CompilerParams(vmem_limit_bytes=8 << 20),
+        cost_estimate=pl.CostEstimate(
+            flops=4_000_000_000, bytes_accessed=weight.size * 2, transcendentals=0
+        ),
+    )(features, parts)
+
+
+def project_other_kernel(feature_ref, weight_ref, part_ref, out_ref):
+    total = part_ref[...]
+    for k in range(feature_ref.shape[0]):
+        weight = weight_ref[k].reshape(feature_ref.shape[2], out_ref.shape[1])
+        total += jnp.dot(feature_ref[k], weight, preferred_element_type=F32)
+    out_ref[...] = total.astype(BF16)
+
+
+def project_other(features, weight, part):
+    vmem = pl.BlockSpec(memory_space=pltpu.VMEM)
+    return pl.pallas_call(
+        project_other_kernel,
+        in_specs=[vmem] * 3,
+        out_specs=vmem,
+        out_shape=jax.ShapeDtypeStruct(part.shape, BF16),
+        name="project_other",
+        compiler_params=pltpu.CompilerParams(vmem_limit_bytes=8 << 20),
+    )(features, weight, part)
 
 
 def next_tokens(value):
@@ -306,23 +359,21 @@
     per_dev = channels // ways
     near = lax.axis_size("y")
 
-    copies = jnp.broadcast_to(out_weight[None], (lax.axis_size("zh"), *out_weight.shape))
+    product, copies = front(value_in, key_in, out_weight, lax.axis_size("zh"))
     weight_rows = to_each(copies, "zh").reshape(-1, out_weight.shape[1])
     weight = lax.all_gather(weight_rows, ("x", "y"), axis=0, tiled=True)
-    product = (value_in.astype(F32) * key_in.astype(F32)).astype(BF16)
     prior = next_tokens(product)
     bands = short_bands(short_filter)
     mid = short_stage(prior, product, gate_short, bands)
     spread = to_each(mid.reshape(ways, per_dev, tokens), CTX)
-    blocks = in_hbm(long_blocks(long_filter))
+    blocks = long_blocks(long_filter)
     long_part = long_stage(spread, blocks)
     returned = to_each(long_part, CTX).reshape(channels, tokens)
     gated = gate_stage(returned, mid, gate_long, skip_gain[None, :], lax.axis_size("zl"), near)
     own = to_each(gated, "zl")
     other = lax.ppermute(own, "core", [(0, 1), (1, 0)])
-    core = lax.axis_index("core").reshape(1)
-    half = project(own, weight, core, None, near)
-    return project(other, weight, 1 - core, half, near)
+    part, rest = project_own(own, weight, near)
+    return project_other(other, rest, part)
 
 
 def solution(mesh):

time: 151 us -> 146 us (0.967)
  Pallas kernels: 21.4 us -> 19 us
  starting transfers between devices: 25.9 us -> 27.9 us
  blocking collectives: 76.2 us -> 74.4 us
    pallas_call x3 -> x4, Pallas kernels: 11.8 us -> 9.34 us  [the longest x1 4.72 us: long_stage(): pl.pallas_call(conv_kernel, in_specs=[vmem, pl.BlockSpec(memory_space=plt...]
    ppermute x1, starting transfers between devices: 6.24 us -> 8.24 us  [shards(): other = lax.ppermute(own, 'core', [(0, 1), (1, 0)])]
    all_to_all x3, blocking collectives: 76.2 us -> 74.4 us  [to_each(): return lax.all_to_all(parts, axes, 0, 0, tiled=True)]
  transfers between devices with their start and end apart: 4 -> 4, of which waited for: 2 -> 2; matrix products, arithmetic and copies ran while one was open for 1% -> 0% of each run, Pallas kernels for 12% -> 11%
where the time goes in v5:
time: 146 us
  blocking collectives  74.4 us (51%)
  starting transfers between devices  27.9 us (19%)
  Pallas kernels  19 us (13%)
  between operations  13.5 us (9%)
  waiting for transfers between devices  10.1 us (7%)
    all_to_all x3, blocking collectives, to_each(): return lax.all_to_all(parts, axes, 0, 0, tiled=True)  74.4 us
    all_to_all x1, starting transfers between devices, to_each(): return lax.all_to_all(parts, axes, 0, 0, tiled=True)  16.5 us
    all_to_all x1, waiting for transfers between devices, to_each(): return lax.all_to_all(parts, axes, 0, 0, tiled=True)  9.23 us
    ppermute x1, starting transfers between devices, shards(): other = lax.ppermute(own, 'core', [(0, 1), (1, 0)])  8.24 us
    pallas_call x1, Pallas kernels, long_blocks(): pl.pallas_call(toeplitz_kernel, grid=(steps,), in_specs=[pl.BlockSpec((ro...  7.01 us
    pallas_call x1, Pallas kernels, long_stage(): pl.pallas_call(conv_kernel, in_specs=[vmem, pl.BlockSpec(memory_space=plt...  4.72 us
    ppermute x1, starting transfers between devices, next_tokens(): return lax.ppermute(value, CTX, [(s, s + 1) for s in range(size - 1)])  3.21 us
  transfers between devices with their start and end apart: 4, of which 2 were waited for; matrix products, arithmetic and copies ran while one was open for 0% of the time, Pallas kernels for 11%

profile of v5, /device:TPU:1, one launch (start us, length us, event | category | flops | bytes accessed | tf_op | source)
XLA Modules:
  0.0 145.6 jit_solution(12370648680640819234)
XLA Ops:
  6.5 0.0 copy-start
  6.5 0.0 all-gather.2.cloned.1.call-start
  6.5 1.3 front.1
  7.8 29.7 %all_to_all.20 = bf16[4,64,512]{2,1,0:T(8,128)(2,1)} all-to-all(bf16[4,64,512]{2,1,0:T(8,128)(2,1)S(1)} %get-tuple-element.10), channel_id=1, replica_groups=mesh['x'=4,'zh'=4,'y'=4,'zl'=4,'core'=2] {'zh'}, dimensions={0} | all-to-all | bytes 524288 | tf_op jit(solution)/shard_map/all_to_all | solution.py:351
  37.6 0.0 all-gather.2.cloned.1.call-update
  37.6 3.2 %collective-permute-start = (bf16[128,512]{1,0:T(8,128)(2,1)S(1)}, bf16[128,512]{1,0:T(8,128)(2,1)S(1)}, u32[]{:S(2)}, u32[]{:S(2)}) collective-permute-start(bf16[128,512]{1,0:T(8,128)(2,1)S(1)} %get-tuple-element.9.own_ref), channel_id=1, source_target_pairs={{0,8},{8,16},{16,24},{24,32},{32,40},{40,48},{48,56},{56,64},{64,7... | collective-permute-start | bytes 393224 | tf_op jit(solution)/shard_map/ppermute | solution.py:343
  40.8 0.0 copy-start.2
  40.8 0.7 copy-done.2
  41.5 0.4 short_bands.1.band_ref
  41.9 0.9 collective-permute-done.prior_ref
  42.7 0.0 copy-done
  42.7 1.1 short_stage.1.refs_1_
  43.8 16.5 %all-to-all-start = ((bf16[64,8,128]{2,1,0:T(8,128)(2,1)}), bf16[64,8,128]{2,1,0:T(8,128)(2,1)S(1)}, u32[]{:S(2)}, u32[]{:S(2)}) async-start(bf16[64,8,128]{2,1,0:T(8,128)(2,1)} %bitcast), calls=%async_computation | async-start | bytes 262144 | tf_op jit(solution)/shard_map/all_to_all | solution.py:351
  60.3 7.0 %long_blocks.1.blk_hbm = bf16[8,512,1024]{2,1,0:T(8,128)(2,1)} custom-call(f32[8,8192]{1,0:T(8,128)} %filt_ref.1), custom_call_target="tpu_custom_call" | custom-call | flops 4000000000 | bytes 8388608 | tf_op jit(solution)/shard_map/long_blocks/pallas_call | solution.py:147
  67.3 0.0 copy-start.1
  67.3 0.0 copy-start.3
  67.3 9.2 %all-to-all-done.sig_ref = bf16[64,8,128]{2,1,0:T(8,128)(2,1)S(1)} async-done(((bf16[64,8,128]{2,1,0:T(8,128)(2,1)}), bf16[64,8,128]{2,1,0:T(8,128)(2,1)S(1)}, u32[]{:S(2)}, u32[]{:S(2)}) %all-to-all-start) | async-done | bytes 131104 | tf_op jit(solution)/shard_map/all_to_all | solution.py:351
  76.6 4.7 %long_stage.1 = bf16[64,8,128]{2,1,0:T(8,128)(2,1)S(1)} custom-call(bf16[64,8,128]{2,1,0:T(8,128)(2,1)S(1)} %all-to-all-done.sig_ref, bf16[8,512,1024]{2,1,0:T(8,128)(2,1)} %long_blocks.1.blk_hbm), custom_call_target="tpu_custom_call" | custom-call | flops 8000000000 | bytes 8388608 | tf_op jit(solution)/shard_map/long_stage/pallas_call | solution.py:218
  81.3 23.8 %all_to_all.21 = bf16[64,8,128]{2,1,0:T(8,128)(2,1)S(1)} all-to-all(bf16[64,8,128]{2,1,0:T(8,128)(2,1)S(1)} %long_stage.1), channel_id=1, replica_groups=mesh['x'=4,'zh'=4,'y'=4,'zl'=4,'core'=2] {'x','zh','y'}, dimensions={0} | all-to-all | bytes 262144 | tf_op jit(solution)/shard_map/all_to_all | solution.py:351
  105.1 0.0 copy-done.1
  105.1 0.0 copy-done.3
  105.1 1.2 gate_stage.1
  106.3 20.8 %all_to_all.22.feature_ref = bf16[4,128,512]{2,1,0:T(8,128)(2,1)S(1)} all-to-all(bf16[4,128,512]{2,1,0:T(8,128)(2,1)S(1)} %gate_stage.1), channel_id=1, replica_groups=mesh['x'=4,'zh'=4,'y'=4,'zl'=4,'core'=2] {'zl'}, dimensions={0} | all-to-all | bytes 1048576 | tf_op jit(solution)/shard_map/all_to_all | solution.py:351
  127.1 8.2 %collective-permute-start.1 = (bf16[4,128,512]{2,1,0:T(8,128)(2,1)S(1)}, bf16[4,128,512]{2,1,0:T(8,128)(2,1)S(1)}, u32[]{:S(2)}, u32[]{:S(2)}) collective-permute-start(bf16[4,128,512]{2,1,0:T(8,128)(2,1)S(1)} %all_to_all.22.feature_ref), channel_id=1, source_target_pairs={{0,1},{1,0},{2,3},{3,2},{4,5},{5,4},{6,7},{7,6},{8,9},{9,8},{10,11... | collective-permute-start | bytes 1572872 | tf_op jit(solution)/shard_map/ppermute | solution.py:374
  135.3 0.0 all-gather.2.cloned.1.call-done
  135.4 2.2 %project_own.1 = (f32[128,512]{1,0:T(8,128)S(1)}, bf16[4,4,128,512]{3,2,1,0:T(8,128)(2,1)S(1)}) custom-call(bf16[4,128,512]{2,1,0:T(8,128)(2,1)S(1)} %all_to_all.22.feature_ref, bf16[4,4,2,128,512]{4,3,2,1,0:T(8,128)(2,1)} %bitcast.8), custom_call_target="tpu_custom_call" | custom-call | flops 4000000000 | bytes 4194304 | tf_op jit(solution)/shard_map/project_own/pallas_call | solution.py:301
  137.6 0.0 collective-permute-done.1.feature_ref
  137.6 1.1 project_other.1
Async XLA Ops:
  6.5 36.2 %copy-start = (bf16[128,512]{1,0:T(8,128)(2,1)S(1)}, bf16[128,512]{1,0:T(8,128)(2,1)}, u32[]{:S(2)}) copy-start(bf16[128,512]{1,0:T(8,128)(2,1)} %gate_ref.1) | copy-start | bytes 393220
  6.5 128.8 %all-gather.2.cloned.1.call-start = ((), (), s32[]{:S(2)}) async-start(), calls=%async_computation.4 | async-start | bytes 4456448 | tf_op jit(solution)/shard_map/all_gather | solution.py:364
  37.6 5.1 %collective-permute-start = (bf16[128,512]{1,0:T(8,128)(2,1)S(1)}, bf16[128,512]{1,0:T(8,128)(2,1)S(1)}, u32[]{:S(2)}, u32[]{:S(2)}) collective-permute-start(bf16[128,512]{1,0:T(8,128)(2,1)S(1)} %get-tuple-element.9.own_ref), channel_id=1, source_target_pairs={{0,8},{8,16},{16,24},{24,32},{32,40},{40,48},{48,56},{56,64},{64,7... | collective-permute-start | bytes 393224 | tf_op jit(solution)/shard_map/ppermute | solution.py:343
  40.8 0.7 copy-start.2
  43.8 32.7 %all-to-all-start = ((bf16[64,8,128]{2,1,0:T(8,128)(2,1)}), bf16[64,8,128]{2,1,0:T(8,128)(2,1)S(1)}, u32[]{:S(2)}, u32[]{:S(2)}) async-start(bf16[64,8,128]{2,1,0:T(8,128)(2,1)} %bitcast), calls=%async_computation | async-start | bytes 262144 | tf_op jit(solution)/shard_map/all_to_all | solution.py:351
  67.3 37.8 %copy-start.1 = (bf16[128,512]{1,0:T(8,128)(2,1)S(1)}, bf16[128,512]{1,0:T(8,128)(2,1)}, u32[]{:S(2)}) copy-start(bf16[128,512]{1,0:T(8,128)(2,1)} %refs_2_.1) | copy-start | bytes 393220
  67.3 37.8 %copy-start.3 = (f32[512]{0:T(512)S(1)}, f32[512]{0:T(512)}, u32[]{:S(2)}) copy-start(f32[512]{0:T(512)} %param.14) | copy-start | bytes 6148
  127.1 10.5 %collective-permute-start.1 = (bf16[4,128,512]{2,1,0:T(8,128)(2,1)S(1)}, bf16[4,128,512]{2,1,0:T(8,128)(2,1)S(1)}, u32[]{:S(2)}, u32[]{:S(2)}) collective-permute-start(bf16[4,128,512]{2,1,0:T(8,128)(2,1)S(1)} %all_to_all.22.feature_ref), channel_id=1, source_target_pairs={{0,1},{1,0},{2,3},{3,2},{4,5},{5,4},{6,7},{7,6},{8,9},{9,8},{10,11... | collective-permute-start | bytes 1572872 | tf_op jit(solution)/shard_map/ppermute | solution.py:374
Sparse Core Ops, SparseCore 0:
  37.7 67.1 all-gather.1

commit v6 on v5

--- a/solution.py
+++ b/solution.py
@@ -25,102 +25,60 @@
     return cols >= at
 
 
-def front_kernel(value_hbm, key_hbm, weight_hbm, product_ref, copies_ref, value, key, weight, sems):
-    loads = [
-        pltpu.make_async_copy(source, target, sems.at[0, k])
-        for k, (source, target) in enumerate(
-            ((weight_hbm, weight), (value_hbm, value), (key_hbm, key))
-        )
-    ]
-    for load in loads:
-        load.start()
-    loads[0].wait()
-    sends = [
-        pltpu.make_async_copy(weight, copies_ref.at[k], sems.at[1, k])
-        for k in range(copies_ref.shape[0])
-    ]
+def front_kernel(weight_hbm, copies_ref, weight, sems):
+    count = copies_ref.shape[0]
+    load = pltpu.make_async_copy(weight_hbm, weight, sems.at[count])
+    load.start()
+    load.wait()
+    sends = [pltpu.make_async_copy(weight, copies_ref.at[k], sems.at[k]) for k in range(count)]
     for send in sends:
         send.start()
-    loads[1].wait()
-    loads[2].wait()
-    product_ref[...] = (value[...].astype(F32) * key[...].astype(F32)).astype(BF16)
     for send in sends:
         send.wait()
 
 
-def front(value, key, weight, count):
+def front(weight, count):
     hbm = pl.BlockSpec(memory_space=pltpu.HBM)
     return pl.pallas_call(
         front_kernel,
-        in_specs=[hbm] * 3,
-        out_specs=(pl.BlockSpec(memory_space=pltpu.VMEM), hbm),
-        out_shape=(
-            jax.ShapeDtypeStruct(value.shape, BF16),
-            jax.ShapeDtypeStruct((count, *weight.shape), weight.dtype),
-        ),
+        in_specs=[hbm],
+        out_specs=hbm,
+        out_shape=jax.ShapeDtypeStruct((count, *weight.shape), weight.dtype),
         scratch_shapes=[
-            pltpu.VMEM(value.shape, BF16),
-            pltpu.VMEM(key.shape, BF16),
             pltpu.VMEM(weight.shape, weight.dtype),
-            pltpu.SemaphoreType.DMA((2, max(count, 3))),
+            pltpu.SemaphoreType.DMA((count + 1,)),
         ],
         name="front",
         compiler_params=pltpu.CompilerParams(vmem_limit_bytes=4 << 20),
-    )(in_hbm(value), in_hbm(key), in_hbm(weight))
-
-
-def band_kernel(taps_ref, band_ref):
-    own = upper()
-    taps = taps_ref[...].astype(F32)
-    for g in range(taps_ref.shape[0]):
-        turned = rolled_rows(taps[g : g + 1, :])
-        band_ref[g, :LANES, :] = jnp.where(own, 0.0, turned).astype(BF16)
-        band_ref[g, LANES:, :] = jnp.where(own, turned, 0.0).astype(BF16)
-
-
-def short_bands(short_filter):
-    groups, taps = short_filter.shape
-    return pl.pallas_call(
-        band_kernel,
-        out_shape=jax.ShapeDtypeStruct((groups, 2 * taps, taps), BF16),
-        name="short_bands",
-        compiler_params=pltpu.CompilerParams(vmem_limit_bytes=8 << 20),
-        cost_estimate=pl.CostEstimate(
-            flops=2_000_000_000, bytes_accessed=groups * taps * taps * 4, transcendentals=0
-        ),
-    )(short_filter)
-
-
-def short_kernel(prior_ref, own_ref, gate_ref, band_ref, mid_ref):
-    groups = band_ref.shape[0]
-    channels = own_ref.shape[1]
-    size = channels // groups
-    for b in range(channels // LANES):
+    )(in_hbm(weight))
+
+
+def pack_kernel(value_ref, key_ref, gate_ref, out_ref):
+    rows = out_ref.shape[1] // 2
+    peers = LANES // rows
+    for b in range(value_ref.shape[1] // LANES):
         cols = slice(b * LANES, (b + 1) * LANES)
-        prior = prior_ref[:, cols].astype(F32).T.astype(BF16)
-        own = own_ref[:, cols].astype(F32).T.astype(BF16)
-        gate = gate_ref[:, cols].astype(F32).T
-        both = jnp.concatenate([prior, own], axis=1)
-        for s in range(LANES // size):
-            rows = slice(s * size, (s + 1) * size)
-            out = jnp.dot(
-                both[rows, :], band_ref[b * (LANES // size) + s], preferred_element_type=F32
-            )
-            start = b * LANES + s * size
-            mid_ref[start : start + size, :] = (gate[rows, :] * out).astype(BF16)
-
-
-def short_stage(prior, own, gate, band):
-    tokens, channels = own.shape
-    return pl.pallas_call(
-        short_kernel,
-        out_shape=jax.ShapeDtypeStruct((channels, tokens), BF16),
-        name="short_stage",
+        to = slice(b * peers, (b + 1) * peers)
+        product = (value_ref[:, cols].astype(F32) * key_ref[:, cols].astype(F32)).astype(BF16)
+        out_ref[to, :rows, :] = product.astype(F32).T.reshape(peers, rows, LANES).astype(BF16)
+        gate = gate_ref[:, cols].astype(F32).T.reshape(peers, rows, LANES)
+        out_ref[to, rows:, :] = gate.astype(BF16)
+
+
+def pack(value, key, gate, rows):
+    tokens, channels = value.shape
+    vmem = pl.BlockSpec(memory_space=pltpu.VMEM)
+    return pl.pallas_call(
+        pack_kernel,
+        in_specs=[vmem] * 3,
+        out_specs=vmem,
+        out_shape=jax.ShapeDtypeStruct((channels // rows, 2 * rows, tokens), BF16),
+        name="pack",
         compiler_params=pltpu.CompilerParams(vmem_limit_bytes=16 << 20),
         cost_estimate=pl.CostEstimate(
-            flops=1_000_000_000, bytes_accessed=4 << 20, transcendentals=0
-        ),
-    )(prior, own, gate, band)
+            flops=1_000_000_000, bytes_accessed=1 << 20, transcendentals=0
+        ),
+    )(value, key, gate)
 
 
 def toeplitz_kernel(filt_ref, out_ref, last):
@@ -198,30 +156,54 @@
     return even + jnp.where(low, turned_down(odd, 1, at), odd)
 
 
-def conv_kernel(sig_ref, blk_hbm, out_ref, sig, acc, blk, sems):
-    count, rows = sig_ref.shape[0], sig_ref.shape[1]
+def ctx_index():
+    at = 0
+    for axis in CTX:
+        at = at * lax.axis_size(axis) + lax.axis_index(axis)
+    return at
+
+
+def conv_kernel(size, sig_ref, taps_ref, skip_ref, blk_hbm, out_ref, sig, acc, blk, sems):
+    count, rows = out_ref.shape[0], out_ref.shape[1]
     loads = [pltpu.make_async_copy(blk_hbm.at[c], blk.at[c], sems.at[c]) for c in range(rows)]
     for load in loads:
         load.start()
-    sig[...] = sig_ref[...].reshape(count * rows, LANES).astype(F32)
+    me = ctx_index()
+    sig[...] = sig_ref[...].reshape(count * 2 * rows, LANES).astype(F32)
+    taps = taps_ref[...].astype(F32)
+    group = lax.broadcasted_iota(jnp.int32, taps.shape, 0) == me * rows // size
+    turned = rolled_rows(jnp.sum(jnp.where(group, taps, 0.0), axis=0, keepdims=True))
+    own = upper()
+    band = jnp.concatenate([jnp.where(own, 0.0, turned), jnp.where(own, turned, 0.0)], axis=0)
+    band = band.astype(BF16)
+    at = lax.broadcasted_iota(jnp.int32, (count, LANES), 0)
+    lane = lax.broadcasted_iota(jnp.int32, skip_ref.shape, 1)
     for c in range(rows):
-        at = pl.ds(c, count, stride=rows)
-        u = sig[at, :]
+        product = sig[pl.ds(c, count, stride=2 * rows), :]
+        gate = sig[pl.ds(rows + c, count, stride=2 * rows), :]
+        both = jnp.concatenate([turned_down(product, 1, at), product], axis=1).astype(BF16)
+        short = jnp.dot(both, band, preferred_element_type=F32)
+        mid = (gate * short).astype(BF16).astype(F32)
         loads[c].wait()
-        acc[at, :] = conv_channel(u, blk, c)
+        far = conv_channel(mid, blk, c).astype(BF16).astype(F32)
+        skip = jnp.sum(
+            jnp.where(lane == me * rows + c, skip_ref[...], 0.0), axis=1, keepdims=True
+        )
+        acc[pl.ds(c, count, stride=rows), :] = far + skip * mid
     out_ref[...] = acc[...].reshape(count, rows, LANES).astype(BF16)
 
 
-def long_stage(signal, blocks):
-    count, rows, _ = signal.shape
+def long_stage(signal, taps, skip, blocks, size):
+    count, twice, _ = signal.shape
+    rows = twice // 2
     vmem = pl.BlockSpec(memory_space=pltpu.VMEM)
     return pl.pallas_call(
-        conv_kernel,
-        in_specs=[vmem, pl.BlockSpec(memory_space=pltpu.HBM)],
+        lambda *refs: conv_kernel(size, *refs),
+        in_specs=[vmem, vmem, vmem, pl.BlockSpec(memory_space=pltpu.HBM)],
         out_specs=vmem,
-        out_shape=jax.ShapeDtypeStruct(signal.shape, BF16),
+        out_shape=jax.ShapeDtypeStruct((count, rows, LANES), BF16),
         scratch_shapes=[
-            pltpu.VMEM((count * rows, LANES), F32),
+            pltpu.VMEM((count * twice, LANES), F32),
             pltpu.VMEM((count * rows, LANES), F32),
             pltpu.VMEM(blocks.shape, BF16),
             pltpu.SemaphoreType.DMA((rows,)),
@@ -231,18 +213,17 @@
         cost_estimate=pl.CostEstimate(
             flops=8_000_000_000, bytes_accessed=blocks.size * 2, transcendentals=0
         ),
-    )(signal, in_hbm(blocks))
-
-
-def gate_kernel(near, long_ref, mid_ref, gate_ref, skip_ref, out_ref):
+    )(signal, taps, skip, in_hbm(blocks))
+
+
+def gate_kernel(near, long_ref, gate_ref, out_ref):
     channels = gate_ref.shape[1]
     tiles = []
     for b in range(channels // LANES):
         rows = slice(b * LANES, (b + 1) * LANES)
         whole = long_ref[rows, :].astype(F32).T
-        mid = mid_ref[rows, :].astype(F32).T
         gate = gate_ref[:, rows].astype(F32)
-        tiles.append(gate * (whole + skip_ref[:, rows] * mid))
+        tiles.append(gate * whole)
     half = LANES // 2
     low = lax.broadcasted_iota(jnp.int32, tiles[0].shape, 1) < half
 
@@ -256,7 +237,7 @@
             out_ref[copy, :, y * LANES : (y + 1) * LANES] = both
 
 
-def gate_stage(long_rows, mid_rows, gate, skip, copies, near):
+def gate_stage(long_rows, gate, copies, near):
     tokens, channels = gate.shape
     return pl.pallas_call(
         lambda *refs: gate_kernel(near, *refs),
@@ -266,7 +247,7 @@
         cost_estimate=pl.CostEstimate(
             flops=1_000_000_000, bytes_accessed=1 << 20, transcendentals=0
         ),
-    )(long_rows, mid_rows, gate, skip)
+    )(long_rows, gate)
 
 
 def project_own_kernel(feature_ref, weight_ref, part_ref, rest_ref, held, sems):
@@ -338,11 +319,6 @@
     )(features, weight, part)
 
 
-def next_tokens(value):
-    size = lax.axis_size(CTX)
-    return lax.ppermute(value, CTX, [(s, s + 1) for s in range(size - 1)])
-
-
 def in_hbm(value):
     return pltpu.with_memory_space_constraint(value, pltpu.HBM)
 
@@ -359,17 +335,17 @@
     per_dev = channels // ways
     near = lax.axis_size("y")
 
-    product, copies = front(value_in, key_in, out_weight, lax.axis_size("zh"))
+    copies = front(out_weight, lax.axis_size("zh"))
     weight_rows = to_each(copies, "zh").reshape(-1, out_weight.shape[1])
     weight = lax.all_gather(weight_rows, ("x", "y"), axis=0, tiled=True)
-    prior = next_tokens(product)
-    bands = short_bands(short_filter)
-    mid = short_stage(prior, product, gate_short, bands)
-    spread = to_each(mid.reshape(ways, per_dev, tokens), CTX)
+    packed = pack(value_in, key_in, gate_short, per_dev)
+    spread = to_each(packed, CTX)
     blocks = long_blocks(long_filter)
-    long_part = long_stage(spread, blocks)
+    long_part = long_stage(
+        spread, short_filter, skip_gain[None, :], blocks, channels // short_filter.shape[0]
+    )
     returned = to_each(long_part, CTX).reshape(channels, tokens)
-    gated = gate_stage(returned, mid, gate_long, skip_gain[None, :], lax.axis_size("zl"), near)
+    gated = gate_stage(returned, gate_long, lax.axis_size("zl"), near)
     own = to_each(gated, "zl")
     other = lax.ppermute(own, "core", [(0, 1), (1, 0)])
     part, rest = project_own(own, weight, near)

time: 146 us -> 135 us (0.925)
  starting transfers between devices: 27.9 us -> 19.5 us
  blocking collectives: 74.4 us -> 70.4 us
  local copies, waits for them, and re-layouts: 0.7 us -> 2.72 us
    all_to_all x1, starting transfers between devices: 16.5 us -> 11.5 us  [to_each(): return lax.all_to_all(parts, axes, 0, 0, tiled=True)]
    all_to_all x3, blocking collectives: 74.4 us -> 70.4 us  [to_each(): return lax.all_to_all(parts, axes, 0, 0, tiled=True)]
    ppermute x1 -> x0, starting transfers between devices: 3.21 us -> none  [next_tokens(): return lax.ppermute(value, CTX, [(s, s + 1) for s in range(size - 1)])]
    unnamed x8 -> x12, local copies, waits for them, and re-layouts: 0.7 us -> 2.72 us
    pallas_call x4 -> x3, Pallas kernels: 7.47 us -> 7.07 us  [the longest x1 5.03 us: long_stage(): pl.pallas_call(lambda *refs: conv_kernel(size, *refs), in_specs=[vmem, vm...]
  transfers between devices with their start and end apart: 4 -> 3, of which waited for: 2 -> 1; matrix products, arithmetic and copies ran while one was open for 0% -> 0% of each run, Pallas kernels for 11% -> 11%
where the time goes in v6:
time: 135 us; the launch traced here: 134 us
  blocking collectives  70.4 us (52%)
  starting transfers between devices  19.5 us (14%)
  Pallas kernels  17.6 us (13%)
  between operations  13.5 us (10%)
  waiting for transfers between devices  10.4 us (8%)
  local copies, waits for them, and re-layouts  2.72 us (2%)
    all_to_all x3, blocking collectives, to_each(): return lax.all_to_all(parts, axes, 0, 0, tiled=True)  70.4 us
    all_to_all x1, starting transfers between devices, to_each(): return lax.all_to_all(parts, axes, 0, 0, tiled=True)  11.5 us
    all_to_all x1, waiting for transfers between devices, to_each(): return lax.all_to_all(parts, axes, 0, 0, tiled=True)  10.3 us
    ppermute x1, starting transfers between devices, shards(): other = lax.ppermute(own, 'core', [(0, 1), (1, 0)])  7.99 us
    pallas_call x1, Pallas kernels, long_blocks(): pl.pallas_call(toeplitz_kernel, grid=(steps,), in_specs=[pl.BlockSpec((ro...  7 us
    pallas_call x1, Pallas kernels, long_stage(): pl.pallas_call(lambda *refs: conv_kernel(size, *refs), in_specs=[vmem, vm...  5.03 us
    unnamed x12, local copies, waits for them, and re-layouts  2.72 us
  transfers between devices with their start and end apart: 3, of which 1 were waited for; matrix products, arithmetic and copies ran while one was open for 0% of the time, Pallas kernels for 11%

profile of v6, /device:TPU:1, one launch (start us, length us, event | category | flops | bytes accessed | tf_op | source)
XLA Modules:
  0.0 134.1 jit_solution(1337403429690070994)
XLA Ops:
  6.5 0.0 all-gather.2.cloned.1.call-start
  6.5 1.2 front.1
  7.7 29.7 %all_to_all.20 = bf16[4,64,512]{2,1,0:T(8,128)(2,1)} all-to-all(bf16[4,64,512]{2,1,0:T(8,128)(2,1)S(1)} %front.1), channel_id=1, replica_groups=mesh['x'=4,'zh'=4,'y'=4,'zl'=4,'core'=2] {'zh'}, dimensions={0} | all-to-all | bytes 524288 | tf_op jit(solution)/shard_map/all_to_all | solution.py:327
  37.5 0.0 all-gather.2.cloned.1.call-update
  37.5 0.0 copy-start
  37.5 0.9 copy-done
  38.4 0.0 copy-start.1
  38.4 0.9 copy-done.1
  39.3 0.0 copy-start.2
  39.3 0.9 copy-done.2
  40.2 0.8 pack.1
  41.1 11.5 %all-to-all-start = ((bf16[64,16,128]{2,1,0:T(8,128)(2,1)}), bf16[64,16,128]{2,1,0:T(8,128)(2,1)S(1)}, u32[]{:S(2)}, u32[]{:S(2)}) async-start(bf16[64,16,128]{2,1,0:T(8,128)(2,1)} %pack.1), calls=%async_computation | async-start | bytes 524288 | tf_op jit(solution)/shard_map/all_to_all | solution.py:327
  52.6 0.0 copy-start.4
  52.6 0.0 copy-start.5
  52.6 7.0 %long_blocks.1.refs_3_ = bf16[8,512,1024]{2,1,0:T(8,128)(2,1)} custom-call(f32[8,8192]{1,0:T(8,128)} %filt_ref.1), custom_call_target="tpu_custom_call" | custom-call | flops 4000000000 | bytes 8388608 | tf_op jit(solution)/shard_map/long_blocks/pallas_call | solution.py:105
  59.6 10.3 %all-to-all-done.refs_0_ = bf16[64,16,128]{2,1,0:T(8,128)(2,1)S(1)} async-done(((bf16[64,16,128]{2,1,0:T(8,128)(2,1)}), bf16[64,16,128]{2,1,0:T(8,128)(2,1)S(1)}, u32[]{:S(2)}, u32[]{:S(2)}) %all-to-all-start) | async-done | bytes 262176 | tf_op jit(solution)/shard_map/all_to_all | solution.py:327
  70.0 0.0 copy-done.4
  70.0 0.0 copy-done.5
  70.0 0.0 copy-start.3
  70.0 5.0 %long_stage.1 = bf16[64,8,128]{2,1,0:T(8,128)(2,1)S(1)} custom-call(bf16[64,16,128]{2,1,0:T(8,128)(2,1)S(1)} %all-to-all-done.refs_0_, bf16[32,128]{1,0:T(8,128)(2,1)S(1)} %copy-done.4, f32[1,512]{1,0:T(1,128)S(1)} %bitcast.5, bf16[8,512,1024]{2,1,0:T(8,128)(2,1)} %long_blocks.1.refs_3_), custom_call_target="tpu_custom_call" | custom-call | flops 8000000000 | bytes 8388608 | tf_op jit(solution)/shard_map/long_stage/pallas_call | solution.py:200
  75.0 22.7 %all_to_all.21 = bf16[64,8,128]{2,1,0:T(8,128)(2,1)S(1)} all-to-all(bf16[64,8,128]{2,1,0:T(8,128)(2,1)S(1)} %long_stage.1), channel_id=1, replica_groups=mesh['x'=4,'zh'=4,'y'=4,'zl'=4,'core'=2] {'x','zh','y'}, dimensions={0} | all-to-all | bytes 262144 | tf_op jit(solution)/shard_map/all_to_all | solution.py:327
  97.7 0.0 copy-done.3
  97.7 0.2 gate_stage.1
  98.0 17.9 %all_to_all.22.feature_ref = bf16[4,128,512]{2,1,0:T(8,128)(2,1)S(1)} all-to-all(bf16[4,128,512]{2,1,0:T(8,128)(2,1)S(1)} %gate_stage.1), channel_id=1, replica_groups=mesh['x'=4,'zh'=4,'y'=4,'zl'=4,'core'=2] {'zl'}, dimensions={0} | all-to-all | bytes 1048576 | tf_op jit(solution)/shard_map/all_to_all | solution.py:327
  115.9 8.0 %collective-permute-start = (bf16[4,128,512]{2,1,0:T(8,128)(2,1)S(1)}, bf16[4,128,512]{2,1,0:T(8,128)(2,1)S(1)}, u32[]{:S(2)}, u32[]{:S(2)}) collective-permute-start(bf16[4,128,512]{2,1,0:T(8,128)(2,1)S(1)} %all_to_all.22.feature_ref), channel_id=1, source_target_pairs={{0,1},{1,0},{2,3},{3,2},{4,5},{5,4},{6,7},{7,6},{8,9},{9,8},{10,11... | collective-permute-start | bytes 1572872 | tf_op jit(solution)/shard_map/ppermute | solution.py:350
  123.9 0.0 all-gather.2.cloned.1.call-done
  123.9 2.2 %project_own.1 = (f32[128,512]{1,0:T(8,128)S(1)}, bf16[4,4,128,512]{3,2,1,0:T(8,128)(2,1)S(1)}) custom-call(bf16[4,128,512]{2,1,0:T(8,128)(2,1)S(1)} %all_to_all.22.feature_ref, bf16[4,4,2,128,512]{4,3,2,1,0:T(8,128)(2,1)} %bitcast.7), custom_call_target="tpu_custom_call" | custom-call | flops 4000000000 | bytes 4194304 | tf_op jit(solution)/shard_map/project_own/pallas_call | solution.py:282
  126.1 0.0 collective-permute-done.feature_ref
  126.1 1.1 project_other.1
Async XLA Ops:
  6.5 117.3 %all-gather.2.cloned.1.call-start = ((), (), s32[]{:S(2)}) async-start(), calls=%async_computation.4 | async-start | bytes 4456448 | tf_op jit(solution)/shard_map/all_gather | solution.py:340
  37.5 0.9 copy-start
  38.4 0.9 copy-start.1
  39.3 0.9 copy-start.2
  41.1 28.9 %all-to-all-start = ((bf16[64,16,128]{2,1,0:T(8,128)(2,1)}), bf16[64,16,128]{2,1,0:T(8,128)(2,1)S(1)}, u32[]{:S(2)}, u32[]{:S(2)}) async-start(bf16[64,16,128]{2,1,0:T(8,128)(2,1)} %pack.1), calls=%async_computation | async-start | bytes 524288 | tf_op jit(solution)/shard_map/all_to_all | solution.py:327
  52.6 17.3 %copy-start.4 = (bf16[32,128]{1,0:T(8,128)(2,1)S(1)}, bf16[32,128]{1,0:T(8,128)(2,1)}, u32[]{:S(2)}) copy-start(bf16[32,128]{1,0:T(8,128)(2,1)} %refs_1_.2) | copy-start | bytes 24580
  52.6 17.3 %copy-start.5 = (f32[512]{0:T(512)S(1)}, f32[512]{0:T(512)}, u32[]{:S(2)}) copy-start(f32[512]{0:T(512)} %param.14) | copy-start | bytes 6148
  70.0 27.8 %copy-start.3 = (bf16[128,512]{1,0:T(8,128)(2,1)S(1)}, bf16[128,512]{1,0:T(8,128)(2,1)}, u32[]{:S(2)}) copy-start(bf16[128,512]{1,0:T(8,128)(2,1)} %refs_1_.3) | copy-start | bytes 393220
  115.9 10.3 %collective-permute-start = (bf16[4,128,512]{2,1,0:T(8,128)(2,1)S(1)}, bf16[4,128,512]{2,1,0:T(8,128)(2,1)S(1)}, u32[]{:S(2)}, u32[]{:S(2)}) collective-permute-start(bf16[4,128,512]{2,1,0:T(8,128)(2,1)S(1)} %all_to_all.22.feature_ref), channel_id=1, source_target_pairs={{0,1},{1,0},{2,3},{3,2},{4,5},{5,4},{6,7},{7,6},{8,9},{9,8},{10,11... | collective-permute-start | bytes 1572872 | tf_op jit(solution)/shard_map/ppermute | solution.py:350
Sparse Core Ops, SparseCore 0:
  37.6 68.4 all-gather.1

commit v7 on v6

--- a/solution.py
+++ b/solution.py
@@ -25,35 +25,17 @@
     return cols >= at
 
 
-def front_kernel(weight_hbm, copies_ref, weight, sems):
-    count = copies_ref.shape[0]
-    load = pltpu.make_async_copy(weight_hbm, weight, sems.at[count])
-    load.start()
-    load.wait()
-    sends = [pltpu.make_async_copy(weight, copies_ref.at[k], sems.at[k]) for k in range(count)]
-    for send in sends:
-        send.start()
-    for send in sends:
-        send.wait()
-
-
-def front(weight, count):
-    hbm = pl.BlockSpec(memory_space=pltpu.HBM)
-    return pl.pallas_call(
-        front_kernel,
-        in_specs=[hbm],
-        out_specs=hbm,
-        out_shape=jax.ShapeDtypeStruct((count, *weight.shape), weight.dtype),
-        scratch_shapes=[
-            pltpu.VMEM(weight.shape, weight.dtype),
-            pltpu.SemaphoreType.DMA((count + 1,)),
-        ],
-        name="front",
-        compiler_params=pltpu.CompilerParams(vmem_limit_bytes=4 << 20),
-    )(in_hbm(weight))
-
-
-def pack_kernel(value_ref, key_ref, gate_ref, out_ref):
+def pack_kernel(value_hbm, key_hbm, gate_hbm, out_ref, value_ref, key_ref, gate_ref, sems):
+    loads = [
+        pltpu.make_async_copy(source, target, sems.at[k])
+        for k, (source, target) in enumerate(
+            ((value_hbm, value_ref), (key_hbm, key_ref), (gate_hbm, gate_ref))
+        )
+    ]
+    for load in loads:
+        load.start()
+    for load in loads:
+        load.wait()
     rows = out_ref.shape[1] // 2
     peers = LANES // rows
     for b in range(value_ref.shape[1] // LANES):
@@ -67,18 +49,18 @@
 
 def pack(value, key, gate, rows):
     tokens, channels = value.shape
-    vmem = pl.BlockSpec(memory_space=pltpu.VMEM)
     return pl.pallas_call(
         pack_kernel,
-        in_specs=[vmem] * 3,
-        out_specs=vmem,
+        in_specs=[pl.BlockSpec(memory_space=pltpu.HBM)] * 3,
+        out_specs=pl.BlockSpec(memory_space=pltpu.VMEM),
+        scratch_shapes=[pltpu.VMEM(value.shape, BF16)] * 3 + [pltpu.SemaphoreType.DMA((3,))],
         out_shape=jax.ShapeDtypeStruct((channels // rows, 2 * rows, tokens), BF16),
         name="pack",
         compiler_params=pltpu.CompilerParams(vmem_limit_bytes=16 << 20),
         cost_estimate=pl.CostEstimate(
             flops=1_000_000_000, bytes_accessed=1 << 20, transcendentals=0
         ),
-    )(value, key, gate)
+    )(in_hbm(value), in_hbm(key), in_hbm(gate))
 
 
 def toeplitz_kernel(filt_ref, out_ref, last):
@@ -335,8 +317,7 @@
     per_dev = channels // ways
     near = lax.axis_size("y")
 
-    copies = front(out_weight, lax.axis_size("zh"))
-    weight_rows = to_each(copies, "zh").reshape(-1, out_weight.shape[1])
+    weight_rows = lax.all_gather(out_weight, "zh", axis=0, tiled=True)
     weight = lax.all_gather(weight_rows, ("x", "y"), axis=0, tiled=True)
     packed = pack(value_in, key_in, gate_short, per_dev)
     spread = to_each(packed, CTX)

time: 135 us -> 128 us (0.948)
  blocking collectives: 70.4 us -> 61.9 us
  waiting for transfers between devices: 10.4 us -> 14.3 us
  local copies, waits for them, and re-layouts: 2.72 us -> 0.02 us
    all_to_all x3 -> x2, blocking collectives: 70.4 us -> 36.1 us  [to_each(): return lax.all_to_all(parts, axes, 0, 0, tiled=True)]
    all_gather x0 -> x1, blocking collectives: none -> 25.8 us  [shards(): weight_rows = lax.all_gather(out_weight, 'zh', axis=0, tiled=True)]
    all_to_all x1, waiting for transfers between devices: 10.3 us -> 14.3 us  [to_each(): return lax.all_to_all(parts, axes, 0, 0, tiled=True)]
    unnamed x12 -> x6, local copies, waits for them, and re-layouts: 2.72 us -> 0.02 us
  transfers between devices with their start and end apart: 3 -> 3, of which waited for: 1 -> 1; matrix products, arithmetic and copies ran while one was open for 0% -> 0% of each run, Pallas kernels for 11% -> 13%
where the time goes in v7:
time: 128 us; the launch traced here: 127 us
  blocking collectives  61.9 us (48%)
  starting transfers between devices  19.9 us (16%)
  Pallas kernels  17.4 us (14%)
  waiting for transfers between devices  14.3 us (11%)
  between operations  13.5 us (11%)
    all_to_all x2, blocking collectives, to_each(): return lax.all_to_all(parts, axes, 0, 0, tiled=True)  36.1 us
    all_gather x1, blocking collectives, shards(): weight_rows = lax.all_gather(out_weight, 'zh', axis=0, tiled=True)  25.8 us
    all_to_all x1, waiting for transfers between devices, to_each(): return lax.all_to_all(parts, axes, 0, 0, tiled=True)  14.3 us
    all_to_all x1, starting transfers between devices, to_each(): return lax.all_to_all(parts, axes, 0, 0, tiled=True)  12.5 us
    ppermute x1, starting transfers between devices, shards(): other = lax.ppermute(own, 'core', [(0, 1), (1, 0)])  7.44 us
    pallas_call x1, Pallas kernels, long_blocks(): pl.pallas_call(toeplitz_kernel, grid=(steps,), in_specs=[pl.BlockSpec((ro...  6.97 us
    pallas_call x1, Pallas kernels, long_stage(): pl.pallas_call(lambda *refs: conv_kernel(size, *refs), in_specs=[vmem, vm...  5.03 us
  transfers between devices with their start and end apart: 3, of which 1 were waited for; matrix products, arithmetic and copies ran while one was open for 0% of the time, Pallas kernels for 13%

profile of v7, /device:TPU:1, one launch (start us, length us, event | category | flops | bytes accessed | tf_op | source)
XLA Modules:
  0.0 127.0 jit_solution(13528222917851620730)
XLA Ops:
  6.5 0.0 all-gather.2.cloned.1.call-start
  6.5 25.8 %all_gather.6 = bf16[256,512]{1,0:T(8,128)(2,1)} all-gather(bf16[64,512]{1,0:T(8,128)(2,1)} %param.15), channel_id=1, replica_groups=mesh['x'=4,'zh'=4,'y'=4,'zl'=4,'core'=2] {'zh'}, dimensions={0}, use_global_device_ids=true | all-gather | bytes 327680 | tf_op jit(solution)/shard_map/all_gather | solution.py:320
  32.3 0.0 all-gather.2.cloned.1.call-update
  32.3 1.9 %pack.1 = bf16[64,16,128]{2,1,0:T(8,128)(2,1)} custom-call(bf16[128,512]{1,0:T(8,128)(2,1)} %value_hbm.1, bf16[128,512]{1,0:T(8,128)(2,1)} %key_hbm.1, bf16[128,512]{1,0:T(8,128)(2,1)} %gate_hbm.1), custom_call_target="tpu_custom_call" | custom-call | flops 1000000000 | bytes 1048576 | tf_op jit(solution)/shard_map/pack/pallas_call | solution.py:52
  34.3 12.5 %all-to-all-start = ((bf16[64,16,128]{2,1,0:T(8,128)(2,1)}), bf16[64,16,128]{2,1,0:T(8,128)(2,1)S(1)}, u32[]{:S(2)}, u32[]{:S(2)}) async-start(bf16[64,16,128]{2,1,0:T(8,128)(2,1)} %pack.1), calls=%async_computation | async-start | bytes 524288 | tf_op jit(solution)/shard_map/all_to_all | solution.py:309
  46.8 0.0 copy-start.1
  46.8 0.0 copy-start.2
  46.8 7.0 %long_blocks.1.refs_3_ = bf16[8,512,1024]{2,1,0:T(8,128)(2,1)} custom-call(f32[8,8192]{1,0:T(8,128)} %filt_ref.1), custom_call_target="tpu_custom_call" | custom-call | flops 4000000000 | bytes 8388608 | tf_op jit(solution)/shard_map/long_blocks/pallas_call | solution.py:87
  53.7 14.3 %all-to-all-done.refs_0_ = bf16[64,16,128]{2,1,0:T(8,128)(2,1)S(1)} async-done(((bf16[64,16,128]{2,1,0:T(8,128)(2,1)}), bf16[64,16,128]{2,1,0:T(8,128)(2,1)S(1)}, u32[]{:S(2)}, u32[]{:S(2)}) %all-to-all-start) | async-done | bytes 262176 | tf_op jit(solution)/shard_map/all_to_all | solution.py:309
  68.0 0.0 copy-done.1
  68.0 0.0 copy-done.2
  68.0 0.0 copy-start
  68.0 5.0 %long_stage.1 = bf16[64,8,128]{2,1,0:T(8,128)(2,1)S(1)} custom-call(bf16[64,16,128]{2,1,0:T(8,128)(2,1)S(1)} %all-to-all-done.refs_0_, bf16[32,128]{1,0:T(8,128)(2,1)S(1)} %copy-done.1, f32[1,512]{1,0:T(1,128)S(1)} %bitcast.4, bf16[8,512,1024]{2,1,0:T(8,128)(2,1)} %long_blocks.1.refs_3_), custom_call_target="tpu_custom_call" | custom-call | flops 8000000000 | bytes 8388608 | tf_op jit(solution)/shard_map/long_stage/pallas_call | solution.py:182
  73.1 22.7 %all_to_all.15 = bf16[64,8,128]{2,1,0:T(8,128)(2,1)S(1)} all-to-all(bf16[64,8,128]{2,1,0:T(8,128)(2,1)S(1)} %long_stage.1), channel_id=1, replica_groups=mesh['x'=4,'zh'=4,'y'=4,'zl'=4,'core'=2] {'x','zh','y'}, dimensions={0} | all-to-all | bytes 262144 | tf_op jit(solution)/shard_map/all_to_all | solution.py:309
  95.8 0.0 copy-done
  95.8 0.2 gate_stage.1
  96.0 13.3 %all_to_all.16.feature_ref = bf16[4,128,512]{2,1,0:T(8,128)(2,1)S(1)} all-to-all(bf16[4,128,512]{2,1,0:T(8,128)(2,1)S(1)} %gate_stage.1), channel_id=1, replica_groups=mesh['x'=4,'zh'=4,'y'=4,'zl'=4,'core'=2] {'zl'}, dimensions={0} | all-to-all | bytes 1048576 | tf_op jit(solution)/shard_map/all_to_all | solution.py:309
  109.4 7.4 %collective-permute-start = (bf16[4,128,512]{2,1,0:T(8,128)(2,1)S(1)}, bf16[4,128,512]{2,1,0:T(8,128)(2,1)S(1)}, u32[]{:S(2)}, u32[]{:S(2)}) collective-permute-start(bf16[4,128,512]{2,1,0:T(8,128)(2,1)S(1)} %all_to_all.16.feature_ref), channel_id=1, source_target_pairs={{0,1},{1,0},{2,3},{3,2},{4,5},{5,4},{6,7},{7,6},{8,9},{9,8},{10,11... | collective-permute-start | bytes 1572872 | tf_op jit(solution)/shard_map/ppermute | solution.py:331
  116.8 0.0 all-gather.2.cloned.1.call-done
  116.8 2.2 %project_own.1 = (f32[128,512]{1,0:T(8,128)S(1)}, bf16[4,4,128,512]{3,2,1,0:T(8,128)(2,1)S(1)}) custom-call(bf16[4,128,512]{2,1,0:T(8,128)(2,1)S(1)} %all_to_all.16.feature_ref, bf16[4,4,2,128,512]{4,3,2,1,0:T(8,128)(2,1)} %bitcast.5), custom_call_target="tpu_custom_call" | custom-call | flops 4000000000 | bytes 4194304 | tf_op jit(solution)/shard_map/project_own/pallas_call | solution.py:264
  119.1 0.0 collective-permute-done.feature_ref
  119.1 1.1 project_other.1
Async XLA Ops:
  6.5 110.3 %all-gather.2.cloned.1.call-start = ((), (), s32[]{:S(2)}) async-start(), calls=%async_computation.3 | async-start | bytes 4456448 | tf_op jit(solution)/shard_map/all_gather | solution.py:321
  34.3 33.8 %all-to-all-start = ((bf16[64,16,128]{2,1,0:T(8,128)(2,1)}), bf16[64,16,128]{2,1,0:T(8,128)(2,1)S(1)}, u32[]{:S(2)}, u32[]{:S(2)}) async-start(bf16[64,16,128]{2,1,0:T(8,128)(2,1)} %pack.1), calls=%async_computation | async-start | bytes 524288 | tf_op jit(solution)/shard_map/all_to_all | solution.py:309
  46.8 21.3 %copy-start.1 = (bf16[32,128]{1,0:T(8,128)(2,1)S(1)}, bf16[32,128]{1,0:T(8,128)(2,1)}, u32[]{:S(2)}) copy-start(bf16[32,128]{1,0:T(8,128)(2,1)} %refs_1_.2) | copy-start | bytes 24580
  46.8 21.3 %copy-start.2 = (f32[512]{0:T(512)S(1)}, f32[512]{0:T(512)}, u32[]{:S(2)}) copy-start(f32[512]{0:T(512)} %param.14) | copy-start | bytes 6148
  68.0 27.8 %copy-start = (bf16[128,512]{1,0:T(8,128)(2,1)S(1)}, bf16[128,512]{1,0:T(8,128)(2,1)}, u32[]{:S(2)}) copy-start(bf16[128,512]{1,0:T(8,128)(2,1)} %refs_1_.3) | copy-start | bytes 393220
  109.4 9.7 %collective-permute-start = (bf16[4,128,512]{2,1,0:T(8,128)(2,1)S(1)}, bf16[4,128,512]{2,1,0:T(8,128)(2,1)S(1)}, u32[]{:S(2)}, u32[]{:S(2)}) collective-permute-start(bf16[4,128,512]{2,1,0:T(8,128)(2,1)S(1)} %all_to_all.16.feature_ref), channel_id=1, source_target_pairs={{0,1},{1,0},{2,3},{3,2},{4,5},{5,4},{6,7},{7,6},{8,9},{9,8},{10,11... | collective-permute-start | bytes 1572872 | tf_op jit(solution)/shard_map/ppermute | solution.py:331
Sparse Core Ops, SparseCore 0:
  32.5 68.0 all-gather.1
